TPU v7x, 32 devices: a whole 2x2x4 slice. The times are simulated.
32 devices in a mesh: pod: 8 (over z, y), data: 4 (over x, core).
Axes of the slice: x: 2, y: 2, z: 4, core: 2. Of those that a mesh axis runs over, the one named last changes fastest.
Arguments:
- feat_a: bfloat16 [16384, 512], P(('pod', 'data'))
- feat_b: bfloat16 [16384, 512], P(('pod', 'data'))
- w_first: bfloat16 [512, 2048], replicated
- w_second: bfloat16 [2048, 2048], replicated
- w_third: bfloat16 [2048, 2048], replicated
- gain_first: float32 [2048], replicated
- shift_first: float32 [2048], replicated
- gain_second: float32 [2048], replicated
- shift_second: float32 [2048], replicated
- lam_off: float32 [], replicated
Outputs:
- output 1: float32 [], replicated
- output 2: float32 [512, 2048], replicated
- output 3: float32 [2048, 2048], replicated
- output 4: float32 [2048, 2048], replicated
- output 5: float32 [2048], replicated
- output 6: float32 [2048], replicated
- output 7: float32 [2048], replicated
- output 8: float32 [2048], replicated
All inputs are finite; a program needn't handle non-finite values.
Results may differ from a plain program's by a relative error of at most 0.001.
Values are sent between devices in bfloat16 or wider.
A program may use at most 1 GiB of HBM per device.

v0:
```python
import functools
import jax
import jax.numpy as jnp
from jax import lax
from jax.sharding import PartitionSpec as P, NamedSharding

BN_EPS = 1e-5
ROW_AXES = ('pod', 'data')


def batch_norm(pre_act, num_rows):
    local_sums = jnp.stack([jnp.sum(pre_act, axis=1), jnp.sum(pre_act * pre_act, axis=1)])
    totals = lax.psum(local_sums, ROW_AXES) / num_rows
    inv_std = lax.rsqrt(totals[1] - totals[0] * totals[0] + BN_EPS)[:, None, :]
    return (pre_act - totals[0][:, None, :]) * inv_std, inv_std


def run_layer(hidden, weight, gain_vec, shift_vec, num_rows):
    pre_act = jnp.einsum('vnf,fd->vnd', hidden, weight, preferred_element_type=jnp.float32)
    normed, inv_std = batch_norm(pre_act, num_rows)
    post_affine = gain_vec * normed + shift_vec
    return jnp.maximum(post_affine, 0.0).astype(jnp.bfloat16), post_affine, normed, inv_std


def norm_backward(grad_norm, normed, inv_std, num_rows):
    local_sums = jnp.stack([jnp.sum(grad_norm, axis=1), jnp.sum(grad_norm * normed, axis=1)])
    totals = lax.psum(local_sums, ROW_AXES) / num_rows
    return inv_std * (grad_norm - totals[0][:, None, :] - normed * totals[1][:, None, :])


def affine_backward(grad_hid, post_affine, normed, inv_std, gain_vec, num_rows):
    grad_act = jnp.where(post_affine > 0, grad_hid, 0.0)
    local_sums = jnp.stack([jnp.sum(grad_act * normed, axis=1), jnp.sum(grad_act, axis=1)])
    totals = lax.psum(local_sums, ROW_AXES)
    grad_pre = (gain_vec * inv_std) * (grad_act - totals[1][:, None, :] / num_rows - normed * (totals[0][:, None, :] / num_rows))
    return grad_pre.astype(jnp.bfloat16), jnp.sum(totals[0], axis=0), jnp.sum(totals[1], axis=0)


def loss_and_grad(corr_mat, lam_off):
    on_diag = jnp.diagonal(corr_mat)
    total_loss = jnp.sum((1.0 - on_diag) ** 2) + lam_off * (jnp.sum(corr_mat * corr_mat) - jnp.sum(on_diag * on_diag))
    diag_mask = lax.broadcasted_iota(jnp.int32, corr_mat.shape, 0) == lax.broadcasted_iota(jnp.int32, corr_mat.shape, 1)
    grad_corr = jnp.where(diag_mask, -2.0 * (1.0 - corr_mat), 2.0 * lam_off * corr_mat)
    return total_loss, grad_corr.astype(jnp.bfloat16)


def device_step(num_dev, feat_a, feat_b, w_first, w_second, w_third, gain_first, shift_first, gain_second, shift_second, lam_off):
    num_rows = feat_a.shape[0] * num_dev
    both_views = jnp.stack([feat_a, feat_b])
    hid_one, post_one, norm_one, inv_one = run_layer(both_views, w_first, gain_first, shift_first, num_rows)
    hid_two, post_two, norm_two, inv_two = run_layer(hid_one, w_second, gain_second, shift_second, num_rows)
    proj_out = jnp.einsum('vnf,fd->vnd', hid_two, w_third, preferred_element_type=jnp.float32)
    emb_norm, inv_three = batch_norm(proj_out, num_rows)
    emb_bf = emb_norm.astype(jnp.bfloat16)
    corr_part = lax.dot_general(emb_bf[0], emb_bf[1], (((0,), (0,)), ((), ())), preferred_element_type=jnp.float32)
    corr_mat = lax.psum(corr_part, ROW_AXES) / num_rows
    total_loss, grad_corr = loss_and_grad(corr_mat, lam_off)
    grad_emb_a = lax.dot_general(emb_bf[1], grad_corr, (((1,), (1,)), ((), ())), preferred_element_type=jnp.float32)
    grad_emb_b = jnp.dot(emb_bf[0], grad_corr, preferred_element_type=jnp.float32)
    grad_emb = jnp.stack([grad_emb_a, grad_emb_b]) / num_rows
    grad_proj = norm_backward(grad_emb, emb_norm, inv_three, num_rows).astype(jnp.bfloat16)
    grad_third = lax.psum(jnp.einsum('woe,wof->ef', hid_two, grad_proj, preferred_element_type=jnp.float32), ROW_AXES)
    grad_hid_two = jnp.einsum('wof,ef->woe', grad_proj, w_third, preferred_element_type=jnp.float32)
    grad_pre_two, grad_gain_second, grad_shift_second = affine_backward(grad_hid_two, post_two, norm_two, inv_two, gain_second, num_rows)
    grad_second = lax.psum(jnp.einsum('woe,wof->ef', hid_one, grad_pre_two, preferred_element_type=jnp.float32), ROW_AXES)
    grad_hid_one = jnp.einsum('wof,ef->woe', grad_pre_two, w_second, preferred_element_type=jnp.float32)
    grad_pre_one, grad_gain_first, grad_shift_first = affine_backward(grad_hid_one, post_one, norm_one, inv_one, gain_first, num_rows)
    grad_first = lax.psum(jnp.einsum('vnf,vnd->fd', both_views, grad_pre_one, preferred_element_type=jnp.float32), ROW_AXES)
    return (total_loss, grad_first, grad_second, grad_third, grad_gain_first, grad_shift_first, grad_gain_second, grad_shift_second)


def solution(mesh):
    num_dev = mesh.shape['pod'] * mesh.shape['data']
    row_spec = P(ROW_AXES, None)
    repl_spec = P()
    return jax.shard_map(functools.partial(device_step, num_dev), mesh=mesh, in_specs=(row_spec, row_spec, repl_spec, repl_spec, repl_spec, repl_spec, repl_spec, repl_spec, repl_spec, repl_spec), out_specs=(repl_spec, repl_spec, repl_spec, repl_spec, repl_spec, repl_spec, repl_spec, repl_spec), check_vma=False)
```

profile of v0, /device:TPU:0, one launch (start us, length us, event | category | flops | bytes accessed | tf_op | source)
XLA Modules:
  0.0 1273.2 jit_solution(2582901979062720900)
XLA Ops:
  7.2 0.0 copy-start
  7.2 0.0 all-reduce.4.cloned.1.call-start
  7.2 1.5 copy-done
  8.8 6.8 fusion.39
  15.6 42.1 %psum.70 = f32[2,2,2048]{2,1,0:T(2,128)S(1)} all-reduce(f32[2,2,2048]{2,1,0:T(2,128)S(1)} %pad_maximum_fusion.3), channel_id=1, replica_groups=mesh['pod'=8,'data'=4] {'pod','data'}, use_global_device_ids=true, to_apply=%region_2.0 | all-reduce | flops 8192 | bytes 65536 | tf_op jit(solution)/shard_map/psum | solution.py:13
  57.7 0.6 fusion.34
  58.4 15.9 %fusion.38 = (f32[2,2048]{1,0:T(2,128)S(1)}, f32[2,2048]{1,0:T(2,128)S(1)}, f32[2,512,2048]{2,1,0:T(8,128)}) fusion(bf16[2048,2048]{1,0:T(8,128)(2,1)} %param.13, f32[2,512,2048]{2,1,0:T(8,128)} %get-tuple-element.41, f32[2048]{0:T(1024)S(1)} %copy-done.12, f32[2,2048]{1,0:T(2,128)S(1)} %get-tuple-element.36, f32[2,2048]{1,0:T(2,128)S(1)} %slice_bitcast_fusion.13, ...), kind=kOutput, calls=%fused_computation.94 | convolution fusion | flops 8608800768 | bytes 25247744 | tf_op jit(solution)/shard_map/vnf,fd->vnd/dot_general | solution.py:19
  74.3 40.4 %psum.71 = f32[2,2,2048]{2,1,0:T(2,128)S(1)} all-reduce(f32[2,2,2048]{2,1,0:T(2,128)S(1)} %pad_maximum_fusion.4), channel_id=1, replica_groups=mesh['pod'=8,'data'=4] {'pod','data'}, use_global_device_ids=true, to_apply=%region_5.0 | all-reduce | flops 8192 | bytes 65536 | tf_op jit(solution)/shard_map/psum | solution.py:13
  114.7 15.8 %fusion.37 = (f32[2,2048]{1,0:T(2,128)S(1)}, f32[2,2048]{1,0:T(2,128)S(1)}, f32[2,512,2048]{2,1,0:T(8,128)}) fusion(bf16[2048,2048]{1,0:T(8,128)(2,1)} %param.14, f32[2,512,2048]{2,1,0:T(8,128)} %get-tuple-element.42, f32[2048]{0:T(1024)S(1)} %copy-done.11, f32[2,2048]{1,0:T(2,128)S(1)} %get-tuple-element.38, f32[2,2048]{1,0:T(2,128)S(1)} %slice_bitcast_fusion.11, ...), kind=kOutput, calls=%fused_computation.93 | convolution fusion | flops 8608800768 | bytes 25247744 | tf_op jit(solution)/shard_map/vnf,fd->vnd/dot_general | solution.py:52
  130.6 40.0 %psum.72 = f32[2,2,2048]{2,1,0:T(2,128)S(1)} all-reduce(f32[2,2,2048]{2,1,0:T(2,128)S(1)} %pad_maximum_fusion.5), channel_id=1, replica_groups=mesh['pod'=8,'data'=4] {'pod','data'}, use_global_device_ids=true, to_apply=%region_8.0 | all-reduce | flops 8192 | bytes 65536 | tf_op jit(solution)/shard_map/psum | solution.py:13
  170.6 4.6 fusion.8
  175.2 0.0 copy-start.4
  175.2 2.0 copy-done.4
  177.2 8.6 fusion.23
  185.8 0.0 all-reduce.4.cloned.1.call-update
  185.8 0.0 all-reduce.6.cloned.1.call-start
  186.5 277.4 %all-reduce.4.cloned.1.call-done = f32[2048,2048]{1,0:T(8,128)} async-done(((f32[2048,2048]{1,0:T(8,128)}), f32[2048,2048]{1,0:T(8,128)}) %all-reduce.4.cloned.1.call-update) | async-done | bytes 16777232 | tf_op jit(solution)/shard_map/psum | solution.py:56
  463.9 9.7 convolution_bitcast_fusion.3
  473.6 0.0 copy-start.2
  473.6 0.0 slice-start.1
  473.6 10.4 convolution_bitcast_fusion.2
  484.1 0.0 copy-start.3
  484.1 2.3 fusion.13
  486.5 40.6 %psum.74 = f32[2,2,2048]{2,1,0:T(2,128)S(1)} all-reduce(f32[2,2,2048]{2,1,0:T(2,128)S(1)} %pad_maximum_fusion.6), channel_id=1, replica_groups=mesh['pod'=8,'data'=4] {'pod','data'}, use_global_device_ids=true, to_apply=%region_15.16 | all-reduce | flops 8192 | bytes 65536 | tf_op jit(solution)/shard_map/psum | solution.py:27
  527.1 0.0 slice-start.8
  527.1 7.2 multiply_convert_fusion.2
  534.3 0.0 slice-start.9
  534.3 16.1 %multiply_reduce_fusion.2 = (f32[2,2048]{1,0:T(2,128)S(1)}, f32[2,2048]{1,0:T(2,128)S(1)}, f32[2,512,2048]{2,1,0:T(8,128)}) fusion(f32[2,512,2048]{2,1,0:T(8,128)} %get-tuple-element.42, f32[2,2048]{1,0:T(2,128)S(1)} %get-tuple-element.38, f32[2,2048]{1,0:T(2,128)S(1)} %slice_bitcast_fusion.11, bf16[2,512,2048]{2,1,0:T(8,128)(2,1)S(1)} %multiply_convert_fusion.2, ...), kind=kOutput, calls=%fused_computation.18 | convolution fusion | flops 8608800768 | bytes 29442048 | tf_op jit(solution)/shard_map/wof,ef->woe/dot_general | solution.py:63
  550.5 12.1 convolution_bitcast_fusion
  562.6 39.5 %psum.75 = f32[2,2,2048]{2,1,0:T(2,128)S(1)} all-reduce(f32[2,2,2048]{2,1,0:T(2,128)S(1)} %pad_maximum_fusion.7), channel_id=1, replica_groups=mesh['pod'=8,'data'=4] {'pod','data'}, use_global_device_ids=true, to_apply=%region_18.19 | all-reduce | flops 8192 | bytes 65536 | tf_op jit(solution)/shard_map/psum | solution.py:34
  602.0 0.6 slice_reduce_fusion.3
  602.7 7.2 multiply_convert_fusion.1
  609.9 16.1 %multiply_reduce_fusion.1 = (f32[2,2048]{1,0:T(2,128)S(1)}, f32[2,2048]{1,0:T(2,128)S(1)}, f32[2,512,2048]{2,1,0:T(8,128)}) fusion(f32[2,512,2048]{2,1,0:T(8,128)} %get-tuple-element.41, f32[2,2048]{1,0:T(2,128)S(1)} %get-tuple-element.36, f32[2,2048]{1,0:T(2,128)S(1)} %slice_bitcast_fusion.13, bf16[2,512,2048]{2,1,0:T(8,128)(2,1)S(1)} %multiply_convert_fusion.1, ...), kind=kOutput, calls=%fused_computation.16 | convolution fusion | flops 8608800768 | bytes 29442048 | tf_op jit(solution)/shard_map/wof,ef->woe/dot_general | solution.py:66
  626.1 0.0 copy-start.6
  626.1 0.0 copy-start.7
  626.1 12.1 convolution_bitcast_fusion.1
  638.3 41.4 %psum.76 = f32[2,2,2048]{2,1,0:T(2,128)S(1)} all-reduce(f32[2,2,2048]{2,1,0:T(2,128)S(1)} %pad_maximum_fusion.8), channel_id=1, replica_groups=mesh['pod'=8,'data'=4] {'pod','data'}, use_global_device_ids=true, to_apply=%region_21.22 | all-reduce | flops 8192 | bytes 65536 | tf_op jit(solution)/shard_map/psum | solution.py:34
  679.6 0.6 slice_reduce_fusion.1
  680.3 10.4 fusion.20
  690.7 0.0 all-reduce.6.cloned.1.call-update
  690.7 13.5 %multiply_reduce_fusion = (f32[]{:T(128)}, f32[2048,2048]{1,0:T(8,128)}) fusion(f32[2048,2048]{1,0:T(8,128)} %all-reduce.4.cloned.1.call-done), kind=kLoop, calls=%fused_computation.3 | loop fusion | flops 12582911 | bytes 33554436 | tf_op jit(solution)/shard_map/reduce_sum | solution.py:41
  704.2 34.0 %gather_fusion = f32[2048]{0:T(1024)S(1)} fusion(f32[2048,2048]{1,0:T(8,128)} %get-tuple-element.30, s32[2048]{0:T(1024)S(1)} %bitcast.120), kind=kCustom, calls=%fused_computation | custom fusion | bytes 32768 | tf_op jit(solution)/shard_map/jit(diagonal)/cond/branch_0_fun/gather | solution.py:40
  738.3 0.6 multiply_reduce_fusion.7
  740.7 497.5 %all-reduce.6.cloned.1.call-done = (f32[512,2048]{1,0:T(8,128)}, f32[2048,2048]{1,0:T(8,128)}, f32[2048,2048]{1,0:T(8,128)}) async-done(((f32[512,2048]{1,0:T(8,128)}, f32[2048,2048]{1,0:T(8,128)}, f32[2048,2048]{1,0:T(8,128)}), (f32[512,2048]{1,0:T(8,128)}, f32[2048,2048]{1,0:T(8,128)}, f32[2048,2048]{1,0:T(8,128)})) %all-reduce.6.cloned.1.call-update) | async-done | bytes 37748752 | tf_op jit(solution)/shard_map/psum | solution.py:68
  1238.2 4.8 copy.32
  1243.1 13.6 %copy.33 = f32[2048,2048]{1,0:T(8,128)} copy(f32[2048,2048]{1,0:T(8,128)} %get-tuple-element.48) | data formatting | bytes 33554432
  1256.7 1.7 slice-done.5
  1258.4 6.3 copy.34
  (55 shorter events, 0.3 us)
Async XLA Ops:
  7.2 1.6 copy-start
  7.2 456.7 %all-reduce.4.cloned.1.call-start = ((), (), s32[]{:S(2)}) async-start(), calls=%async_computation | async-start | bytes 33554432 | tf_op jit(solution)/shard_map/psum | solution.py:56
  8.8 49.0 %copy-start.10 = (f32[2048]{0:T(1024)S(1)}, f32[2048]{0:T(1024)}, u32[]{:S(2)}) copy-start(f32[2048]{0:T(1024)} %param.15) | copy-start | bytes 24580
  8.8 49.6 %copy-start.12 = (f32[2048]{0:T(1024)S(1)}, f32[2048]{0:T(1024)}, u32[]{:S(2)}) copy-start(f32[2048]{0:T(1024)} %param.16) | copy-start | bytes 24580
  58.4 56.3 %copy-start.9 = (f32[2048]{0:T(1024)S(1)}, f32[2048]{0:T(1024)}, u32[]{:S(2)}) copy-start(f32[2048]{0:T(1024)} %param.17) | copy-start | bytes 24580
  58.4 56.3 %copy-start.11 = (f32[2048]{0:T(1024)S(1)}, f32[2048]{0:T(1024)}, u32[]{:S(2)}) copy-start(f32[2048]{0:T(1024)} %param.18) | copy-start | bytes 24580
  175.2 2.0 copy-start.4
  185.8 1052.4 %all-reduce.6.cloned.1.call-start = ((), (), s32[]{:S(2)}) async-start(), calls=%async_computation.1 | async-start | bytes 75497472 | tf_op jit(solution)/shard_map/psum | solution.py:68
  463.9 9.7 copy-start.5
  463.9 20.2 %slice-start = ((s8[8388608]{0:T(1024)(128)(4,1)}), s8[4194304]{0:T(1024)(128)(4,1)S(1)}, s32[]{:S(2)}) async-start(s8[8388608]{0:T(1024)(128)(4,1)} %bitcast.121), calls=%async_computation.2 | async-start | bytes 8388608
  473.6 10.5 copy-start.2
  473.6 10.5 slice-start.1
  484.1 2.3 copy-start.3
  527.1 23.4 %slice-start.8 = ((s8[8388608]{0:T(1024)(128)(4,1)}), s8[4194304]{0:T(1024)(128)(4,1)S(1)}, s32[]{:S(2)}) async-start(s8[8388608]{0:T(1024)(128)(4,1)} %bitcast.127), calls=%async_computation.10 | async-start | bytes 8388608
  534.3 16.1 %slice-start.9 = ((s8[8388608]{0:T(1024)(128)(4,1)}), s8[4194304]{0:T(1024)(128)(4,1)S(1)}, s32[]{:S(2)}) async-start(s8[8388608]{0:T(1024)(128)(4,1)} %bitcast.127), calls=%async_computation.11 | async-start | bytes 8388608
  602.7 23.4 %slice-start.6 = ((s8[8388608]{0:T(1024)(128)(4,1)}), s8[4194304]{0:T(1024)(128)(4,1)S(1)}, s32[]{:S(2)}) async-start(s8[8388608]{0:T(1024)(128)(4,1)} %bitcast.125), calls=%async_computation.8 | async-start | bytes 8388608
  609.9 16.1 %slice-start.7 = ((s8[8388608]{0:T(1024)(128)(4,1)}), s8[4194304]{0:T(1024)(128)(4,1)S(1)}, s32[]{:S(2)}) async-start(s8[8388608]{0:T(1024)(128)(4,1)} %bitcast.125), calls=%async_computation.9 | async-start | bytes 8388608
  626.1 54.2 %copy-start.6 = (bf16[512,512]{1,0:T(8,128)(2,1)S(1)}, bf16[512,512]{1,0:T(8,128)(2,1)}, u32[]{:S(2)}) copy-start(bf16[512,512]{1,0:T(8,128)(2,1)} %param.11) | copy-start | bytes 1572868
  626.1 54.2 %copy-start.7 = (bf16[512,512]{1,0:T(8,128)(2,1)S(1)}, bf16[512,512]{1,0:T(8,128)(2,1)}, u32[]{:S(2)}) copy-start(bf16[512,512]{1,0:T(8,128)(2,1)} %param.10) | copy-start | bytes 1572868
  626.1 54.2 %copy-start.8 = (f32[2,2048]{1,0:T(2,128)S(1)}, f32[2,2048]{1,0:T(2,128)}, u32[]{:S(2)}) copy-start(f32[2,2048]{1,0:T(2,128)} %get-tuple-element.35) | copy-start | bytes 49156
  1238.2 18.4 %slice-start.2 = ((s8[16777216]{0:T(1024)(128)(4,1)}), s8[4194304]{0:T(1024)(128)(4,1)S(1)}, s32[]{:S(2)}) async-start(s8[16777216]{0:T(1024)(128)(4,1)} %bitcast.123), calls=%async_computation.4 | async-start | bytes 8388608
  1243.1 13.6 %slice-start.3 = ((s8[16777216]{0:T(1024)(128)(4,1)}), s8[4194304]{0:T(1024)(128)(4,1)S(1)}, s32[]{:S(2)}) async-start(s8[16777216]{0:T(1024)(128)(4,1)} %bitcast.123), calls=%async_computation.5 | async-start | bytes 8388608
  1243.1 13.6 %slice-start.4 = ((s8[16777216]{0:T(1024)(128)(4,1)}), s8[4194304]{0:T(1024)(128)(4,1)S(1)}, s32[]{:S(2)}) async-start(s8[16777216]{0:T(1024)(128)(4,1)} %bitcast.123), calls=%async_computation.6 | async-start | bytes 8388608
  1243.1 15.3 %slice-start.5 = ((s8[16777216]{0:T(1024)(128)(4,1)}), s8[4194304]{0:T(1024)(128)(4,1)S(1)}, s32[]{:S(2)}) async-start(s8[16777216]{0:T(1024)(128)(4,1)} %bitcast.123), calls=%async_computation.7 | async-start | bytes 8388608
  1258.4 6.3 copy-start.1
Sparse Core Ops, SparseCore 0:
  186.0 277.8 all-reduce.3
  690.8 547.3 all-reduce.5
where the time goes:
time: 1280 us; the launch traced here: 1270 us
  waiting for transfers between devices  775 us (61%)
  blocking collectives  244 us (19%)
  matrix products  134 us (10%)
  local copies, waits for them, and re-layouts  64.1 us (5%)
  other arithmetic  37.5 us (3%)
  between operations  18.7 us (1%)
    psum x1, waiting for transfers between devices, device_step(): lax.psum(jnp.einsum('vnf,vnd->fd', both_views, grad_pre_one, preferred_el...  497 us
    psum x1, waiting for transfers between devices, device_step(): corr_mat = lax.psum(corr_part, ROW_AXES) / num_rows  277 us
    psum x3, blocking collectives, batch_norm(): totals = lax.psum(local_sums, ROW_AXES) / num_rows  122 us
    psum x2, blocking collectives, affine_backward(): totals = lax.psum(local_sums, ROW_AXES)  80.8 us
    psum x1, blocking collectives, norm_backward(): totals = lax.psum(local_sums, ROW_AXES) / num_rows  40.6 us
    gather x1, local copies, waits for them, and re-layouts, loss_and_grad(): on_diag = jnp.diagonal(corr_mat)  34 us
    unnamed x49, local copies, waits for them, and re-layouts  30.1 us
  transfers between devices with their start and end apart: 2, of which 2 were waited for; matrix products, arithmetic and copies ran while one was open for 4% of the time, Pallas kernels for 0%

commit v1 on v0

v1 whole, which is shorter than its diff:
```python
import functools
import jax
import jax.numpy as jnp
from jax import lax
from jax.experimental import pallas as pl
from jax.experimental.pallas import tpu as pltpu
from jax.sharding import PartitionSpec as P

BN_EPS = 1e-5
ROW_AXES = ('pod', 'data')
MESH = pl.DeviceIdType.MESH
WIDTH = 2048
QCOLS = WIDTH // 4
CHUNK = 128
BLOCK = CHUNK // 2


def coordinates():
    pod, dat = lax.axis_index('pod'), lax.axis_index('data')
    return lax.div(pod, 2), lax.rem(pod, 2), lax.div(dat, 2), lax.rem(dat, 2)


def device(z, y, x, c):
    return (z * 2 + y, x * 2 + c)


def remote(src, dst, send, recv, dev):
    copy = pltpu.make_async_remote_copy(src_ref=src, dst_ref=dst, send_sem=send, recv_sem=recv, device_id=dev, device_id_type=MESH)
    copy.start()
    return copy


def meet(peers):
    barrier = pltpu.get_barrier_semaphore()
    for dev in peers:
        pl.semaphore_signal(barrier, inc=1, device_id=dev, device_id_type=MESH)
    pl.semaphore_wait(barrier, len(peers))


def stat_kernel(half, v_ref, o_ref, from_core, plane, line, send, recv):
    z, y, x, c = coordinates()
    core_peer = device(z, y, x, 1 - c)
    plane_peers = [device(z, y, 1 - x, c), device(z, 1 - y, x, c), device(z, 1 - y, 1 - x, c)]
    line_peers = [device(lax.rem(z + o, 4), y, x, c) for o in (1, 2, 3)]
    meet([core_peer] + plane_peers + line_peers)
    mine = pl.ds(pl.multiple_of(c * half, 128), half)
    theirs = pl.ds(pl.multiple_of((1 - c) * half, 128), half)
    copies = [remote(v_ref.at[:, theirs], from_core, send.at[0], recv.at[0], core_peer)]
    copies[0].wait_recv()
    spot = y * 2 + x
    plane[spot] = v_ref[:, mine] + from_core[...]
    for i, dev in enumerate(plane_peers):
        copies.append(remote(plane.at[spot], plane.at[spot], send.at[1 + i], recv.at[1 + i], dev))
    for copy in copies[1:4]:
        copy.wait_recv()
    line[z] = (plane[0] + plane[1]) + (plane[2] + plane[3])
    for i, dev in enumerate(line_peers):
        copies.append(remote(line.at[z], line.at[z], send.at[4 + i], recv.at[4 + i], dev))
    for copy in copies[4:7]:
        copy.wait_recv()
    o_ref[:, mine] = (line[0] + line[1]) + (line[2] + line[3])
    copies.append(remote(o_ref.at[:, mine], o_ref.at[:, mine], send.at[7], recv.at[7], core_peer))
    copies[7].wait_recv()
    for copy in copies:
        copy.wait_send()


def sum_stats(values, collective_id):
    rows, width = values.shape
    half = width // 2
    return pl.pallas_call(
        functools.partial(stat_kernel, half),
        out_shape=jax.ShapeDtypeStruct((rows, width), jnp.float32),
        in_specs=[pl.BlockSpec(memory_space=pltpu.VMEM)],
        out_specs=pl.BlockSpec(memory_space=pltpu.VMEM),
        scratch_shapes=[pltpu.VMEM((rows, half), jnp.float32), pltpu.VMEM((4, rows, half), jnp.float32), pltpu.VMEM((4, rows, half), jnp.float32),
                        pltpu.SemaphoreType.DMA((8,)), pltpu.SemaphoreType.DMA((8,))],
        compiler_params=pltpu.CompilerParams(collective_id=collective_id, has_side_effects=True),
    )(values)


def chunk_plan(row_counts, late):
    plan, counts = [], [0, 0]
    for a, rows in enumerate(row_counts):
        for k in range(rows // 2 // CHUNK):
            kind = 1 if len(plan) % late == late - 1 else 0
            plan.append((a, k, kind, counts[kind]))
            counts[kind] += 1
    return plan, counts


def reduce_kernel(row_counts, plan, num_rows, *refs):
    count = len(row_counts)
    make_grad = num_rows is not None
    parts, refs = refs[:count], refs[count:]
    if make_grad:
        lam_ref, refs = refs[0], refs[1:]
    outs, refs = refs[:count], refs[count:]
    if make_grad:
        loss_ref, refs = refs[0], refs[1:]
    own, from_core, recv_first, recv_rows, recv_line, send, recv, core_send, core_recv, local_sem = refs[:10]
    if make_grad:
        shard = refs[10]
    z, y, x, c = coordinates()
    core_peer = device(z, y, x, 1 - c)
    row_peer = {'x': device(z, y, 1 - x, c), 'y': device(z, 1 - y, x, c)}
    row_pos = {'x': x, 'y': y}
    line_peers = [device(lax.rem(z + o, 4), y, x, c) for o in (1, 2, 3)]
    meet([core_peer, row_peer['x'], row_peer['y']] + line_peers)
    chunks = len(plan)
    sends = []
    order = lambda kind, j: (('x', 'y', 'z'), ('y', 'x', 'z'))[j] if kind == 0 else (('x', 'z', 'y'), ('y', 'z', 'x'))[j]
    state = {}

    def start(k):
        a, n, kind, slot = plan[k]
        half = row_counts[a] // 2
        mine = pl.ds(pl.multiple_of(c * half + n * CHUNK, CHUNK), CHUNK)
        theirs = pl.ds(pl.multiple_of((1 - c) * half + n * CHUNK, CHUNK), CHUNK)
        load = pltpu.make_async_copy(parts[a].at[mine], own.at[k], local_sem.at[k, 2])
        load.start()
        copy = remote(parts[a].at[theirs], from_core.at[k], core_send.at[k, 0], core_recv.at[k, 0], core_peer)
        sends.append(copy)
        state[k] = {'load': load, 'core': copy}
        for j in range(2):
            state[k, j] = dict(row=j * BLOCK, rows=BLOCK, col=0, cols=WIDTH)

    def at(k, s):
        return (k, pl.ds(s['row'] if isinstance(s['row'], int) else pl.multiple_of(s['row'], 16), s['rows']),
                pl.ds(s['col'] if isinstance(s['col'], int) else pl.multiple_of(s['col'], QCOLS), s['cols']))

    def landing(k, j, dim, step):
        _, _, kind, slot = plan[k]
        if step == 0:
            return recv_first.at[k, j]
        if dim == 'z':
            return recv_line[kind].at[slot, j]
        return recv_rows[kind].at[slot, j]

    def scatter(k, j, step):
        dim = order(plan[k][2], j)[step]
        s = state[k, j]
        base = 0 if step == 0 else (1 if step == 1 else 2 if order(plan[k][2], j)[1] != 'z' else 4)
        copies = []
        if dim == 'z':
            for i, dev in enumerate(line_peers):
                part = dict(s, col=lax.rem(z + 1 + i, 4) * QCOLS, cols=QCOLS)
                copies.append(remote(own.at[at(k, part)], landing(k, j, dim, step).at[i], send.at[k, j, base + i], recv.at[k, j, base + i], dev))
            s.update(col=z * QCOLS, cols=QCOLS)
        else:
            half = s['rows'] // 2
            part = dict(s, row=s['row'] + (1 - row_pos[dim]) * half, rows=half)
            copies.append(remote(own.at[at(k, part)], landing(k, j, dim, step), send.at[k, j, base], recv.at[k, j, base], row_peer[dim]))
            s.update(row=s['row'] + row_pos[dim] * half, rows=half)
        sends.extend(copies)
        s['copies'] = copies
        s['land'] = landing(k, j, dim, step)

    def absorb(k, j):
        s = state[k, j]
        for copy in s['copies']:
            copy.wait_recv()
        if len(s['copies']) == 3:
            own[at(k, s)] = (own[at(k, s)] + s['land'][0]) + (s['land'][1] + s['land'][2])
        else:
            own[at(k, s)] = own[at(k, s)] + s['land'][...]

    def first(k):
        state[k]['load'].wait()
        state[k]['core'].wait_recv()
        own[k] = own[k] + from_core[k]
        for j in range(2):
            scatter(k, j, 0)

    def middle(step, k):
        for j in range(2):
            absorb(k, j)
            scatter(k, j, step)

    def out_at(k, s):
        a, n, _, _ = plan[k]
        row = c * (row_counts[a] // 2) + n * CHUNK + s['row']
        return outs[a].at[pl.ds(pl.multiple_of(row, 16), s['rows']), pl.ds(s['col'] if isinstance(s['col'], int) else pl.multiple_of(s['col'], QCOLS), s['cols'])]

    def gather(k, j, step):
        dim = order(plan[k][2], j)[2 - step]
        s = state[k, j]
        base = 5 + (0 if step == 0 else 4 if step == 2 else (1 if order(plan[k][2], j)[2] != 'z' else 3))
        src = out_at(k, s) if step else s['src']
        dst = out_at(k, s)
        copies = []
        if dim == 'z':
            for i, dev in enumerate(line_peers):
                copies.append(remote(src, dst, send.at[k, j, base + i], recv.at[k, j, base + i], dev))
            s.update(col=0, cols=WIDTH)
        else:
            copies.append(remote(src, dst, send.at[k, j, base], recv.at[k, j, base], row_peer[dim]))
            s.update(row=s['row'] - row_pos[dim] * s['rows'], rows=2 * s['rows'])
        sends.extend(copies)
        s['copies'] = copies

    def turn(k):
        a, n, _, _ = plan[k]
        for j in range(2):
            absorb(k, j)
            s = state[k, j]
            if make_grad:
                lam = lam_ref[0, 0]
                corr = own[at(k, s)] * (1.0 / num_rows)
                row = c * (row_counts[a] // 2) + n * CHUNK + s['row'] + lax.broadcasted_iota(jnp.int32, corr.shape, 0)
                col = s['col'] + lax.broadcasted_iota(jnp.int32, corr.shape, 1)
                diag = row == col
                miss = 1.0 - corr
                loss = jnp.where(diag, miss * miss, lam * (corr * corr))
                loss_ref[...] = loss if (k == 0 and j == 0) else loss_ref[...] + loss
                shard[k, j] = jnp.where(diag, -2.0 * miss, (2.0 * lam) * corr).astype(jnp.bfloat16)
                s['src'] = shard.at[k, j]
            else:
                s['src'] = own.at[at(k, s)]
            keep = pltpu.make_async_copy(s['src'], out_at(k, s), local_sem.at[k, j])
            keep.start()
            s['keep'] = keep
            gather(k, j, 0)

    def spread(step, k):
        for j in range(2):
            s = state[k, j]
            for copy in s['copies']:
                copy.wait_recv()
            if step == 1:
                s['keep'].wait()
            gather(k, j, step)

    def pair(k):
        a, n, _, _ = plan[k]
        for j in range(2):
            for copy in state[k, j]['copies']:
                copy.wait_recv()
        row = pl.ds(pl.multiple_of(c * (row_counts[a] // 2) + n * CHUNK, CHUNK), CHUNK)
        copy = remote(outs[a].at[row], outs[a].at[row], core_send.at[k, 1], core_recv.at[k, 1], core_peer)
        sends.append(copy)
        state[k]['pair'] = copy

    for k in range(chunks):
        start(k)
    stages = [first, functools.partial(middle, 1), functools.partial(middle, 2), turn, functools.partial(spread, 1), functools.partial(spread, 2), pair]
    for t in range(chunks + len(stages) - 1):
        for i, stage in enumerate(stages):
            if 0 <= t - i < chunks:
                stage(t - i)
    for k in range(chunks):
        state[k]['pair'].wait_recv()
    for copy in sends:
        copy.wait_send()


def reduce_all(parts, collective_id, lam=None, num_rows=None, late=3):
    row_counts = [p.shape[0] for p in parts]
    plan, counts = chunk_plan(row_counts, late)
    chunks = len(plan)
    any_spec = pl.BlockSpec(memory_space=pl.ANY)
    make_grad = lam is not None
    out_type = jnp.bfloat16 if make_grad else jnp.float32
    in_specs = [any_spec] * len(parts)
    out_specs = [any_spec] * len(parts)
    out_shape = [jax.ShapeDtypeStruct(p.shape, out_type) for p in parts]
    args = list(parts)
    if make_grad:
        in_specs.append(pl.BlockSpec(memory_space=pltpu.SMEM))
        args.append(lam.reshape(1, 1))
        out_specs.append(pl.BlockSpec(memory_space=pltpu.VMEM))
        out_shape.append(jax.ShapeDtypeStruct((BLOCK // 4, QCOLS), jnp.float32))
    ab, ef = counts
    f32 = jnp.float32
    scratch = [
        pltpu.VMEM((chunks, CHUNK, WIDTH), f32),
        pltpu.VMEM((chunks, CHUNK, WIDTH), f32),
        pltpu.VMEM((chunks, 2, BLOCK // 2, WIDTH), f32),
        [pltpu.VMEM((ab, 2, BLOCK // 4, WIDTH), f32), pltpu.VMEM((ef, 2, BLOCK // 4, QCOLS), f32)],
        [pltpu.VMEM((ab, 2, 3, BLOCK // 4, QCOLS), f32), pltpu.VMEM((ef, 2, 3, BLOCK // 2, QCOLS), f32)],
        pltpu.SemaphoreType.DMA((chunks, 2, 10)), pltpu.SemaphoreType.DMA((chunks, 2, 10)),
        pltpu.SemaphoreType.DMA((chunks, 2)), pltpu.SemaphoreType.DMA((chunks, 2)), pltpu.SemaphoreType.DMA((chunks, 3)),
    ]
    if make_grad:
        scratch.append(pltpu.VMEM((chunks, 2, BLOCK // 4, QCOLS), jnp.bfloat16))
    return pl.pallas_call(
        functools.partial(reduce_kernel, row_counts, plan, num_rows if make_grad else None),
        out_shape=out_shape, in_specs=in_specs, out_specs=out_specs, scratch_shapes=scratch,
        compiler_params=pltpu.CompilerParams(collective_id=collective_id, has_side_effects=True, vmem_limit_bytes=56 * 1024 * 1024),
    )(*args)


def total_stats(first, second, collective_id):
    local = jnp.concatenate([first, second])
    return sum_stats(local, collective_id).reshape(2, 2, WIDTH)


def batch_norm(pre_act, num_rows):
    totals = total_stats(jnp.sum(pre_act, axis=1), jnp.sum(pre_act * pre_act, axis=1), 0) / num_rows
    inv_std = lax.rsqrt(totals[1] - totals[0] * totals[0] + BN_EPS)[:, None, :]
    return (pre_act - totals[0][:, None, :]) * inv_std, inv_std


def run_layer(hidden, weight, gain_vec, shift_vec, num_rows):
    pre_act = jnp.einsum('vnf,fd->vnd', hidden, weight, preferred_element_type=jnp.float32)
    normed, inv_std = batch_norm(pre_act, num_rows)
    post_affine = gain_vec * normed + shift_vec
    return jnp.maximum(post_affine, 0.0).astype(jnp.bfloat16), post_affine, normed, inv_std


def affine_backward(grad_hid, post_affine, normed, inv_std, gain_vec, num_rows):
    grad_act = jnp.where(post_affine > 0, grad_hid, 0.0)
    totals = total_stats(jnp.sum(grad_act * normed, axis=1), jnp.sum(grad_act, axis=1), 0)
    grad_pre = (gain_vec * inv_std) * (grad_act - totals[1][:, None, :] / num_rows - normed * (totals[0][:, None, :] / num_rows))
    return grad_pre.astype(jnp.bfloat16), jnp.sum(totals[0], axis=0), jnp.sum(totals[1], axis=0)


def device_step(num_dev, feat_a, feat_b, w_first, w_second, w_third, gain_first, shift_first, gain_second, shift_second, lam_off):
    num_rows = feat_a.shape[0] * num_dev
    both_views = jnp.stack([feat_a, feat_b])
    hid_one, post_one, norm_one, inv_one = run_layer(both_views, w_first, gain_first, shift_first, num_rows)
    hid_two, post_two, norm_two, inv_two = run_layer(hid_one, w_second, gain_second, shift_second, num_rows)
    proj_out = jnp.einsum('vnf,fd->vnd', hid_two, w_third, preferred_element_type=jnp.float32)
    emb_norm, inv_three = batch_norm(proj_out, num_rows)
    emb_bf = emb_norm.astype(jnp.bfloat16)
    corr_part = lax.dot_general(emb_bf[0], emb_bf[1], (((0,), (0,)), ((), ())), preferred_element_type=jnp.float32)
    grad_corr, loss_part = reduce_all([corr_part], 2, lam_off, num_rows)
    grad_emb_a = lax.dot_general(emb_bf[1], grad_corr, (((1,), (1,)), ((), ())), preferred_element_type=jnp.float32)
    grad_emb_b = jnp.dot(emb_bf[0], grad_corr, preferred_element_type=jnp.float32)
    grad_emb = jnp.stack([grad_emb_a, grad_emb_b]) / num_rows
    local = jnp.concatenate([jnp.sum(grad_emb, axis=1), jnp.sum(grad_emb * emb_norm, axis=1)])
    extra = jnp.full((4, 256), jnp.sum(loss_part), jnp.float32)
    totals = sum_stats(jnp.concatenate([local, extra], axis=1), 1)
    total_loss = totals[0, WIDTH]
    totals = totals[:, :WIDTH].reshape(2, 2, WIDTH) / num_rows
    grad_proj = (inv_three * (grad_emb - totals[0][:, None, :] - emb_norm * totals[1][:, None, :])).astype(jnp.bfloat16)
    grad_third = jnp.einsum('woe,wof->ef', hid_two, grad_proj, preferred_element_type=jnp.float32)
    grad_hid_two = jnp.einsum('wof,ef->woe', grad_proj, w_third, preferred_element_type=jnp.float32)
    grad_pre_two, grad_gain_second, grad_shift_second = affine_backward(grad_hid_two, post_two, norm_two, inv_two, gain_second, num_rows)
    grad_second = jnp.einsum('woe,wof->ef', hid_one, grad_pre_two, preferred_element_type=jnp.float32)
    grad_hid_one = jnp.einsum('wof,ef->woe', grad_pre_two, w_second, preferred_element_type=jnp.float32)
    grad_pre_one, grad_gain_first, grad_shift_first = affine_backward(grad_hid_one, post_one, norm_one, inv_one, gain_first, num_rows)
    grad_first = jnp.einsum('vnf,vnd->fd', both_views, grad_pre_one, preferred_element_type=jnp.float32)
    (grad_third,) = reduce_all([grad_third], 3)
    grad_second, grad_first = reduce_all([grad_second, grad_first], 4)
    return (total_loss, grad_first, grad_second, grad_third, grad_gain_first, grad_shift_first, grad_gain_second, grad_shift_second)


def solution(mesh):
    num_dev = mesh.shape['pod'] * mesh.shape['data']
    row_spec = P(ROW_AXES, None)
    repl_spec = P()
    return jax.shard_map(functools.partial(device_step, num_dev), mesh=mesh, in_specs=(row_spec, row_spec, repl_spec, repl_spec, repl_spec, repl_spec, repl_spec, repl_spec, repl_spec, repl_spec), out_specs=(repl_spec, repl_spec, repl_spec, repl_spec, repl_spec, repl_spec, repl_spec, repl_spec), check_vma=False)
```

time: 1280 us -> 771 us (0.60)
  waiting for transfers between devices: 775 us -> 0 us
  Pallas kernels: 0 us -> 559 us
  blocking collectives: 244 us -> 0 us
  local copies, waits for them, and re-layouts: 64.1 us -> 29.3 us
  between operations: 18.7 us -> 2.1 us
    psum x2 -> x0, waiting for transfers between devices: 775 us -> none  [the longest x1 497 us: device_step(): lax.psum(jnp.einsum('vnf,vnd->fd', both_views, grad_pre_one, preferred_el...]
    pallas_call x0 -> x9, Pallas kernels: none -> 559 us  [the longest x3 482 us: reduce_all(): pl.pallas_call(functools.partial(reduce_kernel, row_counts, plan, num_row...]
    psum x6 -> x0, blocking collectives: 244 us -> none  [the longest x3 122 us: batch_norm(): totals = lax.psum(local_sums, ROW_AXES) / num_rows]
    gather x1 -> x0, local copies, waits for them, and re-layouts: 34 us -> none  [loss_and_grad(): on_diag = jnp.diagonal(corr_mat)]
    reduce_sum x3 -> x2, other arithmetic: 16.4 us -> 2.84 us  [the longest x1 2.23 us: device_step(): jnp.sum(grad_emb, axis=1)]
  transfers between devices with their start and end apart: 2 -> 0, of which waited for: 2 -> 0; matrix products, arithmetic and copies ran while one was open for 4% -> 0% of each run, Pallas kernels for 0% -> 0%
where the time goes in v1:
time: 771 us; the launch traced here: 760 us
  Pallas kernels  559 us (73%)
  matrix products  137 us (18%)
  other arithmetic  32.3 us (4%)
  local copies, waits for them, and re-layouts  29.3 us (4%)
    pallas_call x3, Pallas kernels, reduce_all(): pl.pallas_call(functools.partial(reduce_kernel, row_counts, plan, num_row...  482 us
    pallas_call x6, Pallas kernels, sum_stats(): pl.pallas_call(functools.partial(stat_kernel, half), out_shape=jax.ShapeD...  76.7 us
    unnamed x49, local copies, waits for them, and re-layouts  28.1 us
    dot_general x2, matrix products, run_layer(): jnp.einsum('vnf,fd->vnd', hidden, weight, preferred_element_type=jnp.floa...  22.8 us
    dot_general x1, matrix products, device_step(): jnp.einsum('wof,ef->woe', grad_proj, w_third, preferred_element_type=jnp....  17.5 us
    dot_general x1, matrix products, device_step(): jnp.einsum('vnf,fd->vnd', hid_two, w_third, preferred_element_type=jnp.fl...  15.8 us

profile of v1, /device:TPU:0, one launch (start us, length us, event | category | flops | bytes accessed | tf_op | source)
XLA Modules:
  0.0 760.3 jit_solution(16978724671723272096)
XLA Ops:
  0.6 0.0 copy-start
  0.7 1.6 copy-done
  2.2 7.0 fusion.36
  9.2 0.6 pad_maximum_fusion.3.v_ref
  9.9 14.9 %shard_map.161 = f32[4,2048]{1,0:T(4,128)} custom-call(f32[4,2048]{1,0:T(4,128)} %pad_maximum_fusion.3.v_ref), custom_call_target="tpu_custom_call" | custom-call | tf_op jit(solution)/shard_map/pallas_call | solution.py:71
  24.8 0.8 broadcast_multiply_fusion.2
  25.6 0.0 copy-start.14
  25.6 15.8 %fusion.35 = (f32[2,2048]{1,0:T(2,128)S(1)}, f32[2,2048]{1,0:T(2,128)S(1)}, f32[2,512,2048]{2,1,0:T(8,128)}) fusion(bf16[2048,2048]{1,0:T(8,128)(2,1)} %param.13, f32[2,512,2048]{2,1,0:T(8,128)} %get-tuple-element.46, f32[2048]{0:T(1024)S(1)} %copy-done.13, f32[2,2048]{1,0:T(2,128)S(1)} %get-tuple-element.37, f32[2,2048]{1,0:T(2,128)S(1)} %get-tuple-element.38, ...), kind=kOutput, calls=%fused_computation.79 | convolution fusion | flops 8608800768 | bytes 25247744 | tf_op jit(solution)/shard_map/vnf,fd->vnd/dot_general | solution.py:305
  41.4 0.6 pad_maximum_fusion.4.v_ref
  42.0 12.8 %shard_map.162 = f32[4,2048]{1,0:T(4,128)} custom-call(f32[4,2048]{1,0:T(4,128)} %pad_maximum_fusion.4.v_ref), custom_call_target="tpu_custom_call" | custom-call | tf_op jit(solution)/shard_map/pallas_call | solution.py:71
  54.9 0.8 broadcast_multiply_fusion.1
  55.7 15.8 %fusion.34 = (f32[2,2048]{1,0:T(2,128)S(1)}, f32[2,2048]{1,0:T(2,128)S(1)}, f32[2,512,2048]{2,1,0:T(8,128)}) fusion(bf16[2048,2048]{1,0:T(8,128)(2,1)} %param.14, f32[2,512,2048]{2,1,0:T(8,128)} %get-tuple-element.47, f32[2048]{0:T(1024)S(1)} %copy-done.14, f32[2,2048]{1,0:T(2,128)S(1)} %get-tuple-element.40, f32[2,2048]{1,0:T(2,128)S(1)} %get-tuple-element.41, ...), kind=kOutput, calls=%fused_computation.78 | convolution fusion | flops 8608800768 | bytes 25247744 | tf_op jit(solution)/shard_map/vnf,fd->vnd/dot_general | solution.py:323
  71.5 0.6 pad_maximum_fusion.5.v_ref
  72.2 12.1 %shard_map.163 = f32[4,2048]{1,0:T(4,128)} custom-call(f32[4,2048]{1,0:T(4,128)} %pad_maximum_fusion.5.v_ref), custom_call_target="tpu_custom_call" | custom-call | tf_op jit(solution)/shard_map/pallas_call | solution.py:71
  84.2 0.8 broadcast_multiply_fusion
  85.0 4.6 fusion.8
  89.6 0.0 copy-start.6
  89.6 2.0 copy-done.6
  91.6 9.0 %fusion.23.refs_0_ = f32[2048,2048]{1,0:T(8,128)} fusion(bf16[2,512,2048]{2,1,0:T(8,128)(2,1)S(1)} %fusion.8), kind=kOutput, calls=%fused_computation.44 | convolution fusion | flops 4294967296 | bytes 20971520 | tf_op jit(solution)/shard_map/dot_general | solution.py:326
  101.3 126.6 %shard_map.164 = (bf16[2048,2048]{1,0:T(8,128)(2,1)}, f32[16,512]{1,0:T(8,128)}) custom-call(f32[2048,2048]{1,0:T(8,128)} %fusion.23.refs_0_, f32[1,1]{1,0:T(1,128)} %bitcast.55.refs_1_), custom_call_target="tpu_custom_call" | custom-call | tf_op jit(solution)/shard_map/pallas_call | solution.py:286
  228.0 7.7 %convolution_bitcast_fusion.2 = f32[1,512,2048]{2,1,0:T(8,128)S(1)} fusion(bf16[2048,2048]{1,0:T(8,128)(2,1)} %get-tuple-element.12, bf16[2,512,2048]{2,1,0:T(8,128)(2,1)} %copy-done.6), kind=kOutput, calls=%fused_computation.38 | convolution fusion | flops 4294967296 | bytes 14680064 | tf_op jit(solution)/shard_map/dot_general | solution.py:329
  235.7 9.1 %convolution_bitcast_fusion.3 = f32[1,512,2048]{2,1,0:T(8,128)S(1)} fusion(bf16[2048,2048]{1,0:T(8,128)(2,1)} %get-tuple-element.12, bf16[2,512,2048]{2,1,0:T(8,128)(2,1)} %copy-done.6), kind=kOutput, calls=%fused_computation.39 | convolution fusion | flops 4294967296 | bytes 14680064 | tf_op jit(solution)/shard_map/dot_general | solution.py:328
  244.9 2.2 fusion.13
  247.2 0.6 reduce_sum.161
  247.8 1.3 select_maximum_fusion.v_ref
  249.1 12.6 %shard_map.165 = f32[4,2304]{1,0:T(4,128)} custom-call(f32[4,2304]{1,0:T(4,128)} %select_maximum_fusion.v_ref), custom_call_target="tpu_custom_call" | custom-call | tf_op jit(solution)/shard_map/pallas_call | solution.py:71
  261.7 1.2 slice.80
  262.9 0.8 slice_multiply_fusion
  263.7 7.1 multiply_convert_fusion.2
  270.8 17.5 %multiply_reduce_fusion.1 = (f32[2,2048]{1,0:T(2,128)S(1)}, f32[2,2048]{1,0:T(2,128)S(1)}, f32[2,512,2048]{2,1,0:T(8,128)}) fusion(f32[2,512,2048]{2,1,0:T(8,128)} %get-tuple-element.47, f32[2,2048]{1,0:T(2,128)S(1)} %get-tuple-element.40, f32[2,2048]{1,0:T(2,128)S(1)} %get-tuple-element.41, bf16[2,512,2048]{2,1,0:T(8,128)(2,1)S(1)} %multiply_convert_fusion.2, ...), kind=kOutput, calls=%fused_computation.14 | convolution fusion | flops 8608800768 | bytes 29442048 | tf_op jit(solution)/shard_map/wof,ef->woe/dot_general | solution.py:338
  288.2 0.6 pad_maximum_fusion.6.v_ref
  288.9 12.3 %shard_map.166 = f32[4,2048]{1,0:T(4,128)} custom-call(f32[4,2048]{1,0:T(4,128)} %pad_maximum_fusion.6.v_ref), custom_call_target="tpu_custom_call" | custom-call | tf_op jit(solution)/shard_map/pallas_call | solution.py:71
  301.2 1.5 slice_reduce_fusion.3
  302.6 7.2 multiply_convert_fusion.1
  309.9 0.0 slice-start.7
  309.9 15.1 %convolution_bitcast_fusion.1.refs_0_ = f32[2048,2048]{1,0:T(8,128)} fusion(bf16[2,512,2048]{2,1,0:T(8,128)(2,1)S(1)} %multiply_convert_fusion.1, f32[2,512,2048]{2,1,0:T(8,128)} %get-tuple-element.46, f32[2048]{0:T(1024)S(1)} %copy-done.13, f32[2,2048]{1,0:T(2,128)S(1)} %get-tuple-element.37, f32[2,2048]{1,0:T(2,128)S(1)} %get-tuple-element.38, ...), kind=kOutput, calls=%fused_computation.1 | convolution fusion | flops 8602517504 | bytes 29409280 | tf_op jit(solution)/shard_map/woe,wof->ef/dot_general | solution.py:340
  325.0 15.0 %multiply_reduce_fusion = (f32[2,2048]{1,0:T(2,128)S(1)}, f32[2,2048]{1,0:T(2,128)S(1)}, f32[2,512,2048]{2,1,0:T(8,128)}) fusion(f32[2,512,2048]{2,1,0:T(8,128)S(1)} %bitcast.61, f32[2,2048]{1,0:T(2,128)S(1)} %get-tuple-element.37, f32[2,2048]{1,0:T(2,128)S(1)} %get-tuple-element.38, bf16[2,512,2048]{2,1,0:T(8,128)(2,1)S(1)} %multiply_convert_fusion.1, ...), kind=kOutput, calls=%fused_computation.12 | convolution fusion | flops 8608800768 | bytes 29442048 | tf_op jit(solution)/shard_map/wof,ef->woe/dot_general | solution.py:341
  340.0 0.6 pad_maximum_fusion.7.v_ref
  340.6 12.0 %shard_map.167 = f32[4,2048]{1,0:T(4,128)} custom-call(f32[4,2048]{1,0:T(4,128)} %pad_maximum_fusion.7.v_ref), custom_call_target="tpu_custom_call" | custom-call | tf_op jit(solution)/shard_map/pallas_call | solution.py:71
  352.6 1.5 slice_reduce_fusion.1
  354.1 10.4 %fusion.20.refs_1_ = f32[512,2048]{1,0:T(8,128)} fusion(f32[2,512,2048]{2,1,0:T(8,128)} %get-tuple-element.50, f32[2,512,2048]{2,1,0:T(8,128)} %get-tuple-element.46, f32[2,2048]{1,0:T(2,128)S(1)} %get-tuple-element.34, f32[2,2048]{1,0:T(2,128)S(1)} %get-tuple-element.35, f32[2,2048]{1,0:T(2,128)S(1)} %get-tuple-element.36, ...), kind=kOutput, calls=%fused_computation.37 | convolution fusion | flops 2162688000 | bytes 22102016 | tf_op jit(solution)/shard_map/vnf,vnd->fd/dot_general | solution.py:343
  364.5 191.5 %shard_map.168 = (f32[2048,2048]{1,0:T(8,128)}, f32[512,2048]{1,0:T(8,128)}) custom-call(f32[2048,2048]{1,0:T(8,128)} %convolution_bitcast_fusion.1.refs_0_, f32[512,2048]{1,0:T(8,128)} %fusion.20.refs_1_), custom_call_target="tpu_custom_call" | custom-call | tf_op jit(solution)/shard_map/pallas_call | solution.py:286
  556.0 15.1 %convolution_bitcast_fusion.refs_0_ = f32[2048,2048]{1,0:T(8,128)} fusion(bf16[2,512,2048]{2,1,0:T(8,128)(2,1)S(1)} %copy-done.5, f32[2,512,2048]{2,1,0:T(8,128)} %get-tuple-element.47, f32[2048]{0:T(1024)S(1)} %copy-done.14, f32[2,2048]{1,0:T(2,128)S(1)} %get-tuple-element.40, f32[2,2048]{1,0:T(2,128)S(1)} %get-tuple-element.41, f32[2048]{0:T(1024)S(1)} %copy-done.12), kind=kOutput, calls=%fused_computation | convolution fusion | flops 8602517504 | bytes 29409280 | tf_op jit(solution)/shard_map/woe,wof->ef/dot_general | solution.py:337
  571.1 164.2 %shard_map.169 = f32[2048,2048]{1,0:T(8,128)} custom-call(f32[2048,2048]{1,0:T(8,128)} %convolution_bitcast_fusion.refs_0_), custom_call_target="tpu_custom_call" | custom-call | tf_op jit(solution)/shard_map/pallas_call | solution.py:286
  735.4 2.1 copy.28
  737.5 14.0 %copy.29 = f32[2048,2048]{1,0:T(8,128)} copy(f32[2048,2048]{1,0:T(8,128)} %get-tuple-element.61) | data formatting | bytes 33554432
  751.5 2.0 slice-done.5
  753.5 6.3 copy.30
  (46 shorter events, 0.2 us)
Async XLA Ops:
  0.6 1.6 copy-start
  2.2 23.3 %copy-start.11 = (f32[2048]{0:T(1024)S(1)}, f32[2048]{0:T(1024)}, u32[]{:S(2)}) copy-start(f32[2048]{0:T(1024)} %param.15) | copy-start | bytes 24580
  2.2 23.3 %copy-start.13 = (f32[2048]{0:T(1024)S(1)}, f32[2048]{0:T(1024)}, u32[]{:S(2)}) copy-start(f32[2048]{0:T(1024)} %param.16) | copy-start | bytes 24580
  25.6 30.1 %copy-start.12 = (f32[2048]{0:T(1024)S(1)}, f32[2048]{0:T(1024)}, u32[]{:S(2)}) copy-start(f32[2048]{0:T(1024)} %param.17) | copy-start | bytes 24580
  25.6 30.1 %copy-start.14 = (f32[2048]{0:T(1024)S(1)}, f32[2048]{0:T(1024)}, u32[]{:S(2)}) copy-start(f32[2048]{0:T(1024)} %param.18) | copy-start | bytes 24580
  89.6 2.0 copy-start.6
  101.3 143.6 %slice-start = ((s8[8388608]{0:T(1024)(128)(4,1)}), s8[4194304]{0:T(1024)(128)(4,1)S(1)}, s32[]{:S(2)}) async-start(s8[8388608]{0:T(1024)(128)(4,1)} %bitcast.56), calls=%async_computation | async-start | bytes 8388608
  228.0 16.9 %slice-start.1 = ((s8[8388608]{0:T(1024)(128)(4,1)}), s8[4194304]{0:T(1024)(128)(4,1)S(1)}, s32[]{:S(2)}) async-start(s8[8388608]{0:T(1024)(128)(4,1)} %bitcast.56), calls=%async_computation.1 | async-start | bytes 8388608
  235.7 9.2 %copy-start.2 = (f32[1,512,2048]{2,1,0:T(8,128)}, f32[1,512,2048]{2,1,0:T(8,128)S(1)}, u32[]{:S(2)}) copy-start(f32[1,512,2048]{2,1,0:T(8,128)S(1)} %convolution_bitcast_fusion.2) | copy-start | bytes 12582916
  244.9 2.3 copy-start.3
  244.9 2.3 copy-start.10
  270.8 17.5 %copy-start.4 = (bf16[2,512,2048]{2,1,0:T(8,128)(2,1)}, bf16[2,512,2048]{2,1,0:T(8,128)(2,1)S(1)}, u32[]{:S(2)}) copy-start(bf16[2,512,2048]{2,1,0:T(8,128)(2,1)S(1)} %multiply_convert_fusion.2) | copy-start | bytes 12582916
  302.6 22.4 %slice-start.6 = ((s8[8388608]{0:T(1024)(128)(4,1)}), s8[4194304]{0:T(1024)(128)(4,1)S(1)}, s32[]{:S(2)}) async-start(s8[8388608]{0:T(1024)(128)(4,1)} %bitcast.60), calls=%async_computation.6 | async-start | bytes 8388608
  309.9 15.1 %slice-start.7 = ((s8[8388608]{0:T(1024)(128)(4,1)}), s8[4194304]{0:T(1024)(128)(4,1)S(1)}, s32[]{:S(2)}) async-start(s8[8388608]{0:T(1024)(128)(4,1)} %bitcast.60), calls=%async_computation.7 | async-start | bytes 8388608
  325.0 29.1 %copy-start.8 = (bf16[512,512]{1,0:T(8,128)(2,1)S(1)}, bf16[512,512]{1,0:T(8,128)(2,1)}, u32[]{:S(2)}) copy-start(bf16[512,512]{1,0:T(8,128)(2,1)} %param.11) | copy-start | bytes 1572868
  325.0 29.1 %copy-start.9 = (bf16[512,512]{1,0:T(8,128)(2,1)S(1)}, bf16[512,512]{1,0:T(8,128)(2,1)}, u32[]{:S(2)}) copy-start(bf16[512,512]{1,0:T(8,128)(2,1)} %param.10) | copy-start | bytes 1572868
  364.5 191.5 %copy-start.5 = (bf16[2,512,2048]{2,1,0:T(8,128)(2,1)S(1)}, bf16[2,512,2048]{2,1,0:T(8,128)(2,1)}, u32[]{:S(2)}) copy-start(bf16[2,512,2048]{2,1,0:T(8,128)(2,1)} %copy-done.4) | copy-start | bytes 12582916
  571.1 164.2 %copy-start.7 = (f32[512,2048]{1,0:T(8,128)S(1)}, f32[512,2048]{1,0:T(8,128)}, u32[]{:S(2)}) copy-start(f32[512,2048]{1,0:T(8,128)} %get-tuple-element.60) | copy-start | bytes 12582916
  735.3 16.2 %slice-start.2 = ((s8[16777216]{0:T(1024)(128)(4,1)}), s8[4194304]{0:T(1024)(128)(4,1)S(1)}, s32[]{:S(2)}) async-start(s8[16777216]{0:T(1024)(128)(4,1)} %bitcast.58), calls=%async_computation.2 | async-start | bytes 8388608
  737.5 14.0 %slice-start.3 = ((s8[16777216]{0:T(1024)(128)(4,1)}), s8[4194304]{0:T(1024)(128)(4,1)S(1)}, s32[]{:S(2)}) async-start(s8[16777216]{0:T(1024)(128)(4,1)} %bitcast.58), calls=%async_computation.3 | async-start | bytes 8388608
  737.5 14.0 %slice-start.4 = ((s8[16777216]{0:T(1024)(128)(4,1)}), s8[4194304]{0:T(1024)(128)(4,1)S(1)}, s32[]{:S(2)}) async-start(s8[16777216]{0:T(1024)(128)(4,1)} %bitcast.58), calls=%async_computation.4 | async-start | bytes 8388608
  737.5 16.0 %slice-start.5 = ((s8[16777216]{0:T(1024)(128)(4,1)}), s8[4194304]{0:T(1024)(128)(4,1)S(1)}, s32[]{:S(2)}) async-start(s8[16777216]{0:T(1024)(128)(4,1)} %bitcast.58), calls=%async_computation.5 | async-start | bytes 8388608
  753.5 6.3 copy-start.1

commit v2 on v1

v2 whole, which is shorter than its diff:
```python
import functools
import jax
import jax.numpy as jnp
from jax import lax
from jax.experimental import pallas as pl
from jax.experimental.pallas import tpu as pltpu
from jax.sharding import PartitionSpec as P

BN_EPS = 1e-5
ROW_AXES = ('pod', 'data')
MESH = pl.DeviceIdType.MESH
WIDTH = 2048
QCOLS = WIDTH // 4
CHUNK = 128
BLOCK = CHUNK // 2


def coordinates():
    pod, dat = lax.axis_index('pod'), lax.axis_index('data')
    return lax.div(pod, 2), lax.rem(pod, 2), lax.div(dat, 2), lax.rem(dat, 2)


def device(z, y, x, c):
    return (z * 2 + y, x * 2 + c)


def remote(src, dst, send, recv, dev):
    copy = pltpu.make_async_remote_copy(src_ref=src, dst_ref=dst, send_sem=send, recv_sem=recv, device_id=dev, device_id_type=MESH)
    copy.start()
    return copy


def meet(peers):
    barrier = pltpu.get_barrier_semaphore()
    for dev in peers:
        pl.semaphore_signal(barrier, inc=1, device_id=dev, device_id_type=MESH)
    pl.semaphore_wait(barrier, len(peers))


class StatSum:
    def __init__(self, half, v_ref, o_ref, from_core, plane, line, send, recv):
        z, y, x, c = coordinates()
        self.core_peer = device(z, y, x, 1 - c)
        self.plane_peers = [device(z, y, 1 - x, c), device(z, 1 - y, x, c), device(z, 1 - y, 1 - x, c)]
        self.line_peers = [device(lax.rem(z + o, 4), y, x, c) for o in (1, 2, 3)]
        self.mine = pl.ds(pl.multiple_of(c * half, 128), half)
        self.theirs = pl.ds(pl.multiple_of((1 - c) * half, 128), half)
        self.spot, self.z = y * 2 + x, z
        self.refs, self.sems, self.copies = (v_ref, o_ref, from_core, plane, line), (send, recv), []

    def peers(self):
        return [self.core_peer] + self.plane_peers + self.line_peers

    def send(self, src, dst, devs):
        for dev in devs:
            i = len(self.copies)
            self.copies.append(remote(src, dst, self.sems[0].at[i], self.sems[1].at[i], dev))

    def arrived(self, first, last):
        for copy in self.copies[first:last]:
            copy.wait_recv()

    def step(self, i):
        v_ref, o_ref, from_core, plane, line = self.refs
        if i == 0:
            self.send(v_ref.at[:, self.theirs], from_core, [self.core_peer])
        elif i == 1:
            self.arrived(0, 1)
            plane[self.spot] = v_ref[:, self.mine] + from_core[...]
            self.send(plane.at[self.spot], plane.at[self.spot], self.plane_peers)
        elif i == 2:
            self.arrived(1, 4)
            line[self.z] = (plane[0] + plane[1]) + (plane[2] + plane[3])
            self.send(line.at[self.z], line.at[self.z], self.line_peers)
        elif i == 3:
            self.arrived(4, 7)
            o_ref[:, self.mine] = (line[0] + line[1]) + (line[2] + line[3])
            self.send(o_ref.at[:, self.mine], o_ref.at[:, self.mine], [self.core_peer])
        else:
            self.arrived(7, 8)
            for copy in self.copies:
                copy.wait_send()


def stat_kernel(half, *refs):
    total = StatSum(half, *refs)
    meet(total.peers())
    for i in range(5):
        total.step(i)


def sum_stats(values, collective_id):
    rows, width = values.shape
    half = width // 2
    return pl.pallas_call(
        functools.partial(stat_kernel, half),
        out_shape=jax.ShapeDtypeStruct((rows, width), jnp.float32),
        in_specs=[pl.BlockSpec(memory_space=pltpu.VMEM)],
        out_specs=pl.BlockSpec(memory_space=pltpu.VMEM),
        scratch_shapes=[pltpu.VMEM((rows, half), jnp.float32), pltpu.VMEM((4, rows, half), jnp.float32), pltpu.VMEM((4, rows, half), jnp.float32),
                        pltpu.SemaphoreType.DMA((8,)), pltpu.SemaphoreType.DMA((8,))],
        compiler_params=pltpu.CompilerParams(collective_id=collective_id, has_side_effects=True),
    )(values)


TAPER = (32, 64, 96)
RING = 1024


def chunk_plan(row_counts, late):
    plan, base = [], 0
    for a, rows in enumerate(row_counts):
        left = rows // 2
        head = list(TAPER) if a == 0 else []
        tail = list(TAPER[::-1]) if a == len(row_counts) - 1 else []
        left -= sum(head) + sum(tail)
        row = 0
        for size in head + [CHUNK] * (left // CHUNK) + ([left % CHUNK] if left % CHUNK else []) + tail:
            plan.append((a, row, base % RING, size // 2, 1 if len(plan) % late == late - 1 else 0))
            row, base = row + size, base + size
    return plan


def reduce_kernel(row_counts, plan, num_rows, work, *refs):
    count = len(row_counts)
    make_grad = num_rows is not None
    if work:
        extra, refs = refs[:WORK_INPUTS], refs[WORK_INPUTS:]
    else:
        parts, refs = refs[:count], refs[count:]
    if make_grad:
        lam_ref, refs = refs[0], refs[1:]
    outs, refs = refs[:count], refs[count:]
    if work:
        parts, extra, refs = refs[:count], extra + refs[:WORK_OUTPUTS], refs[WORK_OUTPUTS:]
    if make_grad:
        loss_ref, refs = refs[0], refs[1:]
    own, from_core, recv_first, recv_second, recv_third, send, recv, core_send, core_recv, local_sem = refs[:10]
    if make_grad:
        shard = refs[10]
        loss_ref[...] = jnp.zeros_like(loss_ref)
    z, y, x, c = coordinates()
    core_peer = device(z, y, x, 1 - c)
    flat_peer = {'x': device(z, y, 1 - x, c), 'y': device(z, 1 - y, x, c)}
    flat_pos = {'x': x, 'y': y}
    line_peers = [device(lax.rem(z + o, 4), y, x, c) for o in (1, 2, 3)]
    plane_peers = [flat_peer['x'], flat_peer['y'], device(z, 1 - y, 1 - x, c)]
    meet([core_peer] + (plane_peers if work else plane_peers[:2]) + line_peers)
    hooks = work(extra + refs[10:]) if work else {}
    chunks = len(plan)
    sends = {}
    order = lambda kind, j: (('x', 'y', 'z'), ('y', 'x', 'z'))[j] if kind == 0 else (('x', 'z', 'y'), ('y', 'z', 'x'))[j]
    state = {}

    def start(k):
        a, row, base, size, _ = plan[k]
        sends[k] = []
        for old in list(sends):
            if old < k and plan[old][2] < base + 2 * size and base < plan[old][2] + 2 * plan[old][3]:
                finish(old)
        half = row_counts[a] // 2
        mine = pl.ds(pl.multiple_of(c * half + row, 16), 2 * size)
        theirs = pl.ds(pl.multiple_of((1 - c) * half + row, 16), 2 * size)
        load = pltpu.make_async_copy(parts[a].at[mine], own.at[pl.ds(base, 2 * size)], local_sem.at[k, 2])
        load.start()
        copy = remote(parts[a].at[theirs], from_core.at[pl.ds(base, 2 * size)], core_send.at[k, 0], core_recv.at[k, 0], core_peer)
        sends[k].append(copy)
        state[k] = {'load': load, 'core': copy}
        for j in range(2):
            state[k, j] = dict(rows=pl.ds(base + j * size, size), out=row + j * size, size=size, col=0, cols=WIDTH)

    def finish(k):
        state[k]['pair'].wait_recv()
        for copy in sends.pop(k):
            copy.wait_send()

    def columns(s):
        return pl.ds(s['col'] if isinstance(s['col'], int) else pl.multiple_of(s['col'], 128), s['cols'])

    def at(s):
        return s['rows'], columns(s)

    def scatter(k, j, step):
        dims = order(plan[k][4], j)
        dim = dims[step]
        s = state[k, j]
        base = 0 if step == 0 else (1 if step == 1 else 2 if dims[1] != 'z' else 4)
        buffer = (recv_first, recv_second, recv_third)[step]
        cols = s['cols'] // (4 if dim == 'z' else 2)
        copies, lands = [], []
        spots = [(lax.rem(z + o, 4), line_peers[o - 1]) for o in (1, 2, 3)] if dim == 'z' else [(1 - flat_pos[dim], flat_peer[dim])]
        for i, (spot, dev) in enumerate(spots):
            land = buffer.at[s['rows'], pl.ds(i * cols, cols)]
            part = dict(s, col=s['col'] + spot * cols, cols=cols)
            copies.append(remote(own.at[at(part)], land, send.at[k, j, base + i], recv.at[k, j, base + i], dev))
            lands.append(land)
        s.update(col=s['col'] + (z if dim == 'z' else flat_pos[dim]) * cols, cols=cols, copies=copies, lands=lands)
        sends[k].extend(copies)

    def absorb(k, j):
        s = state[k, j]
        for copy in s['copies']:
            copy.wait_recv()
        lands = [land[...] for land in s['lands']]
        total = own[at(s)] + lands[0]
        if len(lands) == 3:
            total = total + (lands[1] + lands[2])
        return total

    def first(k):
        _, _, base, size, _ = plan[k]
        state[k]['load'].wait()
        state[k]['core'].wait_recv()
        rows = pl.ds(base, 2 * size)
        own[rows] = own[rows] + from_core[rows]
        for j in range(2):
            scatter(k, j, 0)

    def middle(step, k):
        for j in range(2):
            own[at(state[k, j])] = absorb(k, j)
            scatter(k, j, step)

    def out_at(k, s):
        a = plan[k][0]
        row = c * (row_counts[a] // 2) + s['out']
        return outs[a].at[pl.ds(pl.multiple_of(row, 16), s['size']), columns(s)]

    def gather(k, j, step):
        dims = order(plan[k][4], j)
        dim = dims[2 - step]
        s = state[k, j]
        base = 5 + (0 if step == 0 else 4 if step == 2 else (1 if dims[2] != 'z' else 3))
        src = out_at(k, s) if step else s['src']
        dst = out_at(k, s)
        peers = line_peers if dim == 'z' else [flat_peer[dim]]
        copies = [remote(src, dst, send.at[k, j, base + i], recv.at[k, j, base + i], dev) for i, dev in enumerate(peers)]
        s.update(col=s['col'] - (z if dim == 'z' else flat_pos[dim]) * s['cols'], cols=(4 if dim == 'z' else 2) * s['cols'], copies=copies)
        if step == 2:
            s.update(col=0)
        sends[k].extend(copies)

    def turn(k):
        a = plan[k][0]
        for j in range(2):
            s = state[k, j]
            total = absorb(k, j)
            if make_grad:
                lam = lam_ref[0, 0]
                corr = total * (1.0 / num_rows)
                row = c * (row_counts[a] // 2) + s['out'] + lax.broadcasted_iota(jnp.int32, corr.shape, 0)
                col = s['col'] + lax.broadcasted_iota(jnp.int32, corr.shape, 1)
                diag = row == col
                miss = 1.0 - corr
                loss = jnp.where(diag, miss * miss, lam * (corr * corr))
                loss_ref[...] = loss_ref[...] + jnp.sum(loss.reshape(s['size'] // 8, 8, 128), axis=0)
                shard[s['rows']] = jnp.where(diag, -2.0 * miss, (2.0 * lam) * corr).astype(jnp.bfloat16)
                s['src'] = shard.at[s['rows']]
            else:
                own[at(s)] = total
                s['src'] = own.at[at(s)]
            s['keep'] = pltpu.make_async_copy(s['src'], out_at(k, s), local_sem.at[k, j])
            s['keep'].start()
            gather(k, j, 0)

    def spread(step, k):
        for j in range(2):
            s = state[k, j]
            for copy in s['copies']:
                copy.wait_recv()
            if step == 1:
                s['keep'].wait()
            gather(k, j, step)

    def pair(k):
        a, row, _, size, _ = plan[k]
        for j in range(2):
            for copy in state[k, j]['copies']:
                copy.wait_recv()
        rows = pl.ds(pl.multiple_of(c * (row_counts[a] // 2) + row, 16), 2 * size)
        copy = remote(outs[a].at[rows], outs[a].at[rows], core_send.at[k, 1], core_recv.at[k, 1], core_peer)
        sends[k].append(copy)
        state[k]['pair'] = copy

    stages = [first, functools.partial(middle, 1), functools.partial(middle, 2), turn, functools.partial(spread, 1), functools.partial(spread, 2), pair]
    for t in range(chunks + len(stages) - 1):
        for task in hooks.get(t, ()):
            task()
        for k in range(chunks):
            if t == (max(k - 1, 0) if work and k >= len(TAPER) else 0):
                start(k)
        for i, stage in enumerate(stages):
            if 0 <= t - i < chunks:
                stage(t - i)
    for k in list(sends):
        finish(k)


def reduce_all(parts, collective_id, lam=None, num_rows=None, late=3):
    row_counts = [p.shape[0] for p in parts]
    plan = chunk_plan(row_counts, late)
    chunks, rows = len(plan), sum(row_counts) // 2
    any_spec = pl.BlockSpec(memory_space=pl.ANY)
    make_grad = lam is not None
    out_type = jnp.bfloat16 if make_grad else jnp.float32
    in_specs = [any_spec] * len(parts)
    out_specs = [any_spec] * len(parts)
    out_shape = [jax.ShapeDtypeStruct(p.shape, out_type) for p in parts]
    args = list(parts)
    if make_grad:
        in_specs.append(pl.BlockSpec(memory_space=pltpu.SMEM))
        args.append(lam.reshape(1, 1))
        out_specs.append(pl.BlockSpec(memory_space=pltpu.VMEM))
        out_shape.append(jax.ShapeDtypeStruct((8, 128), jnp.float32))
    f32 = jnp.float32
    scratch = [
        pltpu.VMEM((rows, WIDTH), f32), pltpu.VMEM((rows, WIDTH), f32), pltpu.VMEM((rows, WIDTH // 2), f32),
        pltpu.VMEM((rows, 3 * WIDTH // 8), f32), pltpu.VMEM((rows, 3 * WIDTH // 16), f32),
        pltpu.SemaphoreType.DMA((chunks, 2, 10)), pltpu.SemaphoreType.DMA((chunks, 2, 10)),
        pltpu.SemaphoreType.DMA((chunks, 2)), pltpu.SemaphoreType.DMA((chunks, 2)), pltpu.SemaphoreType.DMA((chunks, 3)),
    ]
    if make_grad:
        scratch.append(pltpu.VMEM((rows, WIDTH // 16), jnp.bfloat16))
    return pl.pallas_call(
        functools.partial(reduce_kernel, row_counts, plan, num_rows if make_grad else None, None),
        out_shape=out_shape, in_specs=in_specs, out_specs=out_specs, scratch_shapes=scratch,
        compiler_params=pltpu.CompilerParams(collective_id=collective_id, has_side_effects=True, vmem_limit_bytes=56 * 1024 * 1024),
    )(*args)


WORK_INPUTS, WORK_OUTPUTS = 9, 5
TILE = 256
VIEW_ROWS = 512


def backward_work(num_rows, refs):
    grad_proj, hid_two, w_third, w_second, pre_two, pre_one, hid_one, feats, vec = refs[:9]
    part_third, part_second, part_first, total_two, total_one = refs[9:14]
    grad, act, w_buf, n_buf, x_buf, o_buf = refs[14:20]
    stat_two, stat_one = refs[20:26], refs[26:32]
    grad_sem, w_sem, n_sem, x_sem, o_sem = refs[32:37]
    rows_of = [pl.ds(v * VIEW_ROWS, VIEW_ROWS) for v in range(2)]
    sums = [StatSum(WIDTH // 2, st[0], tot, *st[1:]) for st, tot in ((stat_two, total_two), (stat_one, total_one))]

    def tile(i):
        return pl.ds(pl.multiple_of(i * TILE, TILE), TILE)

    def loop(first, last, fetch, body):
        for copy in fetch(first, first % 2):
            copy.start()

        def trip(i, carry):
            slot = lax.rem(i, 2)

            @pl.when(i + 1 < last)
            def _():
                for copy in fetch(i + 1, 1 - slot):
                    copy.start()
            for copy in fetch(i, slot):
                copy.wait()
            body(i, slot)
            return carry
        lax.fori_loop(first, last, trip, 0)

    def pre_copy(pre, i, slot):
        return pltpu.make_async_copy(pre.at[:, tile(i)], n_buf.at[slot], n_sem.at[slot])

    def normed(slot, v, first, cols):
        return (n_buf[slot, rows_of[v]] - vec[pl.ds(first + 4 + v, 1), cols]) * vec[pl.ds(first + 2 + v, 1), cols]

    def input_grad(layer, first, last):
        weight, pre = ((w_second, pre_one), (w_third, pre_two))[layer]
        stat = (stat_one, stat_two)[layer][0]
        g = 6 if layer == 0 else 0

        def fetch(i, slot):
            return [pltpu.make_async_copy(weight.at[tile(i)], w_buf.at[slot], w_sem.at[slot]), pre_copy(pre, i, slot)]

        def body(i, slot):
            cols = tile(i)
            for v in range(2):
                dx = lax.dot_general(grad[rows_of[v]], w_buf[slot], (((1,), (1,)), ((), ())), preferred_element_type=jnp.float32)
                n = normed(slot, v, g, cols)
                da = jnp.where(vec[pl.ds(g, 1), cols] * n + vec[pl.ds(g + 1, 1), cols] > 0, dx, 0.0)
                act[rows_of[v], cols] = da
                stat[pl.ds(v, 1), cols] = jnp.sum(da * n, axis=0, keepdims=True)
                stat[pl.ds(2 + v, 1), cols] = jnp.sum(da, axis=0, keepdims=True)
        loop(first, last, fetch, body)

    def norm_grad(layer):
        pre, total = ((pre_one, total_one), (pre_two, total_two))[layer]
        g = 6 if layer == 0 else 0

        def body(i, slot):
            cols = tile(i)
            for v in range(2):
                cross = total[pl.ds(v, 1), cols] * (1.0 / num_rows)
                mean = total[pl.ds(2 + v, 1), cols] * (1.0 / num_rows)
                scale = vec[pl.ds(g, 1), cols] * vec[pl.ds(g + 2 + v, 1), cols]
                grad[rows_of[v], cols] = (scale * (act[rows_of[v], cols] - mean - normed(slot, v, g, cols) * cross)).astype(jnp.bfloat16)
        loop(0, WIDTH // TILE, lambda i, slot: [pre_copy(pre, i, slot)], body)

    def weight_grad(hidden, out, first, last):
        tiles = out.shape[0] // TILE
        spot = lambda i: lax.div(i, 2) + lax.rem(i, 2) * (tiles // 2)

        def fetch(i, slot):
            return [pltpu.make_async_copy(hidden.at[:, tile(spot(i))], x_buf.at[slot], x_sem.at[slot])]

        def put(i, slot):
            return pltpu.make_async_copy(o_buf.at[slot], out.at[tile(spot(i))], o_sem.at[slot])

        def body(i, slot):
            @pl.when(i >= first + 2)
            def _():
                put(i, slot).wait()
            for n in range(4):
                cols = pl.ds(n * (WIDTH // 4), WIDTH // 4)
                o_buf[slot, :, cols] = lax.dot_general(x_buf[slot], grad[:, cols], (((0,), (0,)), ((), ())), preferred_element_type=jnp.float32)
            put(i, slot).start()
        loop(first, last, fetch, body)
        for i in (last - 2, last - 1):
            put(i, i % 2).wait()

    grad_load = pltpu.make_async_copy(grad_proj, grad, grad_sem)
    grad_load.start()
    step = lambda which, i: functools.partial(sums[which].step, i)
    run = functools.partial
    return {
        0: [grad_load.wait, run(weight_grad, hid_two, part_third, 0, 2)], 1: [run(weight_grad, hid_two, part_third, 2, 4)],
        2: [run(weight_grad, hid_two, part_third, 4, 8)], 3: [run(input_grad, 1, 0, 4)], 4: [run(input_grad, 1, 4, 8), step(0, 0)],
        5: [step(0, 1)], 6: [step(0, 2)], 7: [step(0, 3)], 8: [step(0, 4), run(norm_grad, 1)],
        9: [run(weight_grad, hid_one, part_second, 0, 4)], 10: [run(weight_grad, hid_one, part_second, 4, 8)],
        11: [run(input_grad, 0, 0, 4)], 12: [run(input_grad, 0, 4, 8), step(1, 0)],
        13: [step(1, 1)], 14: [step(1, 2)], 15: [step(1, 3)], 16: [step(1, 4), run(norm_grad, 0)], 17: [run(weight_grad, feats, part_first, 0, 2)],
    }


def reduce_with_backward(work_inputs, collective_id, num_rows):
    row_counts = [WIDTH, WIDTH, WIDTH // 4]
    plan = chunk_plan(row_counts, 3)
    chunks, rows, views = len(plan), RING, 2 * VIEW_ROWS
    any_spec, vmem_spec = pl.BlockSpec(memory_space=pl.ANY), pl.BlockSpec(memory_space=pltpu.VMEM)
    f32, bf16, dma = jnp.float32, jnp.bfloat16, pltpu.SemaphoreType.DMA
    half = WIDTH // 2
    stat = [pltpu.VMEM((4, WIDTH), f32), pltpu.VMEM((4, half), f32), pltpu.VMEM((4, 4, half), f32), pltpu.VMEM((4, 4, half), f32), dma((8,)), dma((8,))]
    scratch = [
        pltpu.VMEM((rows, WIDTH), f32), pltpu.VMEM((rows, WIDTH), f32), pltpu.VMEM((rows, WIDTH // 2), f32),
        pltpu.VMEM((rows, 3 * WIDTH // 8), f32), pltpu.VMEM((rows, 3 * WIDTH // 16), f32),
        dma((chunks, 2, 10)), dma((chunks, 2, 10)), dma((chunks, 2)), dma((chunks, 2)), dma((chunks, 3)),
        pltpu.VMEM((views, WIDTH), bf16), pltpu.VMEM((views, WIDTH), f32), pltpu.VMEM((2, TILE, WIDTH), bf16), pltpu.VMEM((2, views, TILE), f32),
        pltpu.VMEM((2, views, TILE), bf16), pltpu.VMEM((2, TILE, WIDTH), f32),
        *stat, *stat, dma, dma((2,)), dma((2,)), dma((2,)), dma((2,)),
    ]
    shape = jax.ShapeDtypeStruct
    return pl.pallas_call(
        functools.partial(reduce_kernel, row_counts, plan, None, functools.partial(backward_work, num_rows)),
        out_shape=[shape((r, WIDTH), f32) for r in row_counts + row_counts] + [shape((4, WIDTH), f32)] * 2,
        in_specs=[any_spec] * 8 + [vmem_spec], out_specs=[any_spec] * 6 + [vmem_spec] * 2, scratch_shapes=scratch,
        compiler_params=pltpu.CompilerParams(collective_id=collective_id, has_side_effects=True, vmem_limit_bytes=62 * 1024 * 1024),
    )(*work_inputs)


def total_stats(first, second, collective_id):
    local = jnp.concatenate([first, second])
    return sum_stats(local, collective_id).reshape(2, 2, WIDTH)


def batch_norm(pre_act, num_rows):
    totals = total_stats(jnp.sum(pre_act, axis=1), jnp.sum(pre_act * pre_act, axis=1), 0) / num_rows
    inv_std = lax.rsqrt(totals[1] - totals[0] * totals[0] + BN_EPS)
    return (pre_act - totals[0][:, None, :]) * inv_std[:, None, :], totals[0], inv_std


def run_layer(hidden, weight, gain_vec, shift_vec, num_rows):
    pre_act = jnp.einsum('vnf,fd->vnd', hidden, weight, preferred_element_type=jnp.float32)
    normed, mean, inv_std = batch_norm(pre_act, num_rows)
    post_affine = gain_vec * normed + shift_vec
    return jnp.maximum(post_affine, 0.0).astype(jnp.bfloat16), pre_act, jnp.concatenate([gain_vec[None], shift_vec[None], inv_std, mean])


def device_step(num_dev, feat_a, feat_b, w_first, w_second, w_third, gain_first, shift_first, gain_second, shift_second, lam_off):
    num_rows = feat_a.shape[0] * num_dev
    both_views = jnp.stack([feat_a, feat_b])
    hid_one, pre_one, vec_one = run_layer(both_views, w_first, gain_first, shift_first, num_rows)
    hid_two, pre_two, vec_two = run_layer(hid_one, w_second, gain_second, shift_second, num_rows)
    proj_out = jnp.einsum('vnf,fd->vnd', hid_two, w_third, preferred_element_type=jnp.float32)
    emb_norm, _, inv_three = batch_norm(proj_out, num_rows)
    inv_three = inv_three[:, None, :]
    emb_bf = emb_norm.astype(jnp.bfloat16)
    corr_part = lax.dot_general(emb_bf[0], emb_bf[1], (((0,), (0,)), ((), ())), preferred_element_type=jnp.float32)
    grad_corr, loss_part = reduce_all([corr_part], 2, lam_off, num_rows)
    grad_emb_a = lax.dot_general(emb_bf[1], grad_corr, (((1,), (1,)), ((), ())), preferred_element_type=jnp.float32)
    grad_emb_b = jnp.dot(emb_bf[0], grad_corr, preferred_element_type=jnp.float32)
    grad_emb = jnp.stack([grad_emb_a, grad_emb_b]) / num_rows
    local = jnp.concatenate([jnp.sum(grad_emb, axis=1), jnp.sum(grad_emb * emb_norm, axis=1)])
    extra = jnp.full((4, 256), jnp.sum(loss_part), jnp.float32)
    totals = sum_stats(jnp.concatenate([local, extra], axis=1), 1)
    total_loss = totals[0, WIDTH]
    totals = totals[:, :WIDTH].reshape(2, 2, WIDTH) / num_rows
    grad_proj = (inv_three * (grad_emb - totals[0][:, None, :] - emb_norm * totals[1][:, None, :])).astype(jnp.bfloat16)
    flat = lambda t: t.reshape(-1, t.shape[-1])
    grad_third, grad_second, grad_first, _, _, _, total_two, total_one = reduce_with_backward(
        [flat(grad_proj), flat(hid_two), w_third, w_second, flat(pre_two), flat(pre_one), flat(hid_one), flat(both_views), jnp.concatenate([vec_two, vec_one])],
        3, num_rows)
    grad_gain_second, grad_shift_second = total_two[0] + total_two[1], total_two[2] + total_two[3]
    grad_gain_first, grad_shift_first = total_one[0] + total_one[1], total_one[2] + total_one[3]
    return (total_loss, grad_first, grad_second, grad_third, grad_gain_first, grad_shift_first, grad_gain_second, grad_shift_second)


def solution(mesh):
    num_dev = mesh.shape['pod'] * mesh.shape['data']
    row_spec = P(ROW_AXES, None)
    repl_spec = P()
    return jax.shard_map(functools.partial(device_step, num_dev), mesh=mesh, in_specs=(row_spec, row_spec, repl_spec, repl_spec, repl_spec, repl_spec, repl_spec, repl_spec, repl_spec, repl_spec), out_specs=(repl_spec, repl_spec, repl_spec, repl_spec, repl_spec, repl_spec, repl_spec, repl_spec), check_vma=False)
```

time: 771 us -> 682 us (0.88)
  matrix products: 137 us -> 63.3 us
  Pallas kernels: 559 us -> 540 us
  other arithmetic: 32.3 us -> 40.8 us
    pallas_call x0 -> x1, Pallas kernels: none -> 362 us  [reduce_with_backward(): pl.pallas_call(functools.partial(reduce_kernel, row_counts, plan, None, f...]
    pallas_call x3 -> x1, Pallas kernels: 482 us -> 126 us  [reduce_all(): pl.pallas_call(functools.partial(reduce_kernel, row_counts, plan, num_row...]
    dot_general x5 -> x0, matrix products: 73 us -> none  [the longest x1 17.5 us: device_step(): jnp.einsum('wof,ef->woe', grad_proj, w_third, preferred_element_type=jnp....]
    pallas_call x6 -> x4, Pallas kernels: 76.7 us -> 52.1 us  [sum_stats(): pl.pallas_call(functools.partial(stat_kernel, half), out_shape=jax.ShapeD...]
    unnamed x49 -> x31, local copies, waits for them, and re-layouts: 28.1 us -> 28.4 us
where the time goes in v2:
time: 682 us; the launch traced here: 677 us
  Pallas kernels  540 us (79%)
  matrix products  63.3 us (9%)
  other arithmetic  40.8 us (6%)
  local copies, waits for them, and re-layouts  30.9 us (5%)
    pallas_call x1, Pallas kernels, reduce_with_backward(): pl.pallas_call(functools.partial(reduce_kernel, row_counts, plan, None, f...  362 us
    pallas_call x1, Pallas kernels, reduce_all(): pl.pallas_call(functools.partial(reduce_kernel, row_counts, plan, num_row...  126 us
    pallas_call x4, Pallas kernels, sum_stats(): pl.pallas_call(functools.partial(stat_kernel, half), out_shape=jax.ShapeD...  52.1 us
    unnamed x31, local copies, waits for them, and re-layouts  28.4 us
    dot_general x2, matrix products, run_layer(): jnp.einsum('vnf,fd->vnd', hidden, weight, preferred_element_type=jnp.floa...  22.6 us
    dot_general x1, matrix products, device_step(): jnp.einsum('vnf,fd->vnd', hid_two, w_third, preferred_element_type=jnp.fl...  14.9 us

profile of v2, /device:TPU:0, one launch (start us, length us, event | category | flops | bytes accessed | tf_op | source)
XLA Modules:
  0.0 677.1 jit_solution(915061218640842004)
XLA Ops:
  1.3 2.4 pad_maximum_fusion
  3.6 7.7 %fusion.17 = (f32[2,2048]{1,0:T(2,128)S(1)}, f32[2,2048]{1,0:T(2,128)S(1)}, f32[2,512,2048]{2,1,0:T(8,128)}) fusion(bf16[512,2048]{1,0:T(8,128)(2,1)} %param.12, bf16[1,512,512]{2,1,0:T(8,128)(2,1)} %bitcast.59, bf16[1,512,512]{2,1,0:T(8,128)(2,1)} %bitcast.61), kind=kOutput, calls=%fused_computation.47 | convolution fusion | flops 2154291200 | bytes 11567104 | tf_op jit(solution)/shard_map/vnf,fd->vnd/dot_general | solution.py:476
  11.4 0.6 pad_maximum_fusion.1.refs_0_
  12.0 14.9 %shard_map.161 = f32[4,2048]{1,0:T(4,128)} custom-call(f32[4,2048]{1,0:T(4,128)} %pad_maximum_fusion.1.refs_0_), custom_call_target="tpu_custom_call" | custom-call | tf_op jit(solution)/shard_map/pallas_call | solution.py:95
  26.9 0.8 broadcast_multiply_fusion.2
  27.7 0.0 copy-done.6
  27.7 0.0 copy-done.7
  27.7 4.9 maximum_convert_fusion.1
  32.6 0.0 copy-start
  32.6 0.0 copy-start.8
  32.7 0.0 copy-start.9
  32.7 14.9 %fusion.16 = (f32[2,2048]{1,0:T(2,128)S(1)}, f32[2,2048]{1,0:T(2,128)S(1)}, f32[2,512,2048]{2,1,0:T(8,128)}) fusion(bf16[2,512,2048]{2,1,0:T(8,128)(2,1)S(1)} %maximum_convert_fusion.1, bf16[2048,2048]{1,0:T(8,128)(2,1)} %refs_3_.1), kind=kOutput, calls=%fused_computation.46 | convolution fusion | flops 8596217856 | bytes 21004288 | tf_op jit(solution)/shard_map/vnf,fd->vnd/dot_general | solution.py:476
  47.6 0.6 pad_maximum_fusion.2.refs_0_
  48.2 12.9 %shard_map.162 = f32[4,2048]{1,0:T(4,128)} custom-call(f32[4,2048]{1,0:T(4,128)} %pad_maximum_fusion.2.refs_0_), custom_call_target="tpu_custom_call" | custom-call | tf_op jit(solution)/shard_map/pallas_call | solution.py:95
  61.1 0.8 broadcast_multiply_fusion.1
  61.9 1.4 concatenate.23.refs_8_
  63.2 4.9 maximum_convert_fusion
  68.2 0.0 copy-start.1
  68.2 14.9 %fusion.15 = (f32[2,2048]{1,0:T(2,128)S(1)}, f32[2,2048]{1,0:T(2,128)S(1)}, f32[2,512,2048]{2,1,0:T(8,128)}) fusion(bf16[2,512,2048]{2,1,0:T(8,128)(2,1)S(1)} %maximum_convert_fusion, bf16[2048,2048]{1,0:T(8,128)(2,1)} %refs_2_.1), kind=kOutput, calls=%fused_computation.45 | convolution fusion | flops 8596217856 | bytes 21004288 | tf_op jit(solution)/shard_map/vnf,fd->vnd/dot_general | solution.py:487
  83.1 0.6 pad_maximum_fusion.3.refs_0_
  83.7 12.1 %shard_map.163 = f32[4,2048]{1,0:T(4,128)} custom-call(f32[4,2048]{1,0:T(4,128)} %pad_maximum_fusion.3.refs_0_), custom_call_target="tpu_custom_call" | custom-call | tf_op jit(solution)/shard_map/pallas_call | solution.py:95
  95.8 0.8 broadcast_multiply_fusion
  96.6 4.6 fusion.4
  101.2 0.0 copy-start.4
  101.2 2.0 copy-done.4
  103.2 8.7 %fusion.8.refs_0_ = f32[2048,2048]{1,0:T(8,128)} fusion(bf16[2,512,2048]{2,1,0:T(8,128)(2,1)S(1)} %fusion.4), kind=kOutput, calls=%fused_computation.21 | convolution fusion | flops 4294967296 | bytes 20971520 | tf_op jit(solution)/shard_map/dot_general | solution.py:491
  112.0 125.7 %shard_map.164 = (bf16[2048,2048]{1,0:T(8,128)(2,1)}, f32[8,128]{1,0:T(8,128)}) custom-call(f32[2048,2048]{1,0:T(8,128)} %fusion.8.refs_0_, f32[1,1]{1,0:T(1,128)} %bitcast.49.refs_1_), custom_call_target="tpu_custom_call" | custom-call | tf_op jit(solution)/shard_map/pallas_call | solution.py:324
  237.7 1.3 reduce_sum.89
  239.0 8.5 %convolution_bitcast_fusion = f32[1,512,2048]{2,1,0:T(8,128)S(1)} fusion(bf16[2048,2048]{1,0:T(8,128)(2,1)} %get-tuple-element.15, bf16[2,512,2048]{2,1,0:T(8,128)(2,1)} %copy-done.4), kind=kOutput, calls=%fused_computation.15 | convolution fusion | flops 4294967296 | bytes 14680064 | tf_op jit(solution)/shard_map/dot_general | solution.py:494
  247.6 0.0 copy-done.5
  247.6 0.0 copy-start.2
  247.6 8.5 %convolution_bitcast_fusion.1 = f32[1,512,2048]{2,1,0:T(8,128)S(1)} fusion(bf16[2048,2048]{1,0:T(8,128)(2,1)} %get-tuple-element.15, bf16[2,512,2048]{2,1,0:T(8,128)(2,1)S(1)} %copy-done.5), kind=kOutput, calls=%fused_computation.16 | convolution fusion | flops 4294967296 | bytes 14680064 | tf_op jit(solution)/shard_map/dot_general | solution.py:493
  256.1 0.0 copy-done.2
  256.1 0.0 copy-start.3
  256.1 6.1 fusion.5
  262.2 0.0 copy-done.3
  262.2 1.3 select_maximum_fusion.refs_0_
  263.4 12.3 %shard_map.165 = f32[4,2304]{1,0:T(4,128)} custom-call(f32[4,2304]{1,0:T(4,128)} %select_maximum_fusion.refs_0_), custom_call_target="tpu_custom_call" | custom-call | tf_op jit(solution)/shard_map/pallas_call | solution.py:95
  275.7 1.2 slice.86
  276.9 0.8 slice_multiply_fusion
  277.7 8.7 %multiply_convert_fusion = bf16[2,512,2048]{2,1,0:T(8,128)(2,1)} fusion(f32[2,512,2048]{2,1,0:T(8,128)} %get-tuple-element.44, f32[1,512,2048]{2,1,0:T(8,128)} %copy-done.2, f32[1,512,2048]{2,1,0:T(8,128)} %copy-done.3, f32[2,2048]{1,0:T(2,128)S(1)} %get-tuple-element.35, f32[2,2048]{1,0:T(2,128)S(1)} %get-tuple-element.34, ...), kind=kLoop, calls=%fused_computation.5 | loop fusion | flops 18874368 | bytes 21037056 | tf_op jit(solution)/shard_map/convert_element_type | solution.py:501
  286.5 362.5 %shard_map.166 = (f32[2048,2048]{1,0:T(8,128)}, f32[2048,2048]{1,0:T(8,128)}, f32[512,2048]{1,0:T(8,128)}, f32[2048,2048]{1,0:T(8,128)}, f32[2048,2048]{1,0:T(8,...) custom-call(bf16[1024,2048]{1,0:T(8,128)(2,1)} %bitcast.52, bf16[1024,2048]{1,0:T(8,128)(2,1)} %bitcast.54, ...), custom_call_target="tpu_custom_call" | custom-call | tf_op jit(solution)/shard_map/pallas_call | solution.py:456
  648.9 1.6 slice_add_fusion
  650.6 4.8 copy.22
  655.4 13.6 %copy.23 = f32[2048,2048]{1,0:T(8,128)} copy(f32[2048,2048]{1,0:T(8,128)} %get-tuple-element.57) | data formatting | bytes 33554432
  669.0 0.0 slice-done.2
  669.0 1.7 slice-done.3
  670.7 6.2 copy.24
  (18 shorter events, 0.1 us)
Async XLA Ops:
  3.6 24.1 %copy-start.6 = (f32[2048]{0:T(1024)S(1)}, f32[2048]{0:T(1024)}, u32[]{:S(2)}) copy-start(f32[2048]{0:T(1024)} %param.16) | copy-start | bytes 24580
  3.6 24.1 %copy-start.7 = (f32[2048]{0:T(1024)S(1)}, f32[2048]{0:T(1024)}, u32[]{:S(2)}) copy-start(f32[2048]{0:T(1024)} %param.15) | copy-start | bytes 24580
  32.6 14.9 %copy-start = (bf16[2,512,2048]{2,1,0:T(8,128)(2,1)}, bf16[2,512,2048]{2,1,0:T(8,128)(2,1)S(1)}, u32[]{:S(2)}) copy-start(bf16[2,512,2048]{2,1,0:T(8,128)(2,1)S(1)} %maximum_convert_fusion.1) | copy-start | bytes 12582916
  32.6 29.2 %copy-start.8 = (f32[2048]{0:T(1024)S(1)}, f32[2048]{0:T(1024)}, u32[]{:S(2)}) copy-start(f32[2048]{0:T(1024)} %param.18) | copy-start | bytes 24580
  32.7 29.2 %copy-start.9 = (f32[2048]{0:T(1024)S(1)}, f32[2048]{0:T(1024)}, u32[]{:S(2)}) copy-start(f32[2048]{0:T(1024)} %param.17) | copy-start | bytes 24580
  68.2 15.0 %copy-start.1 = (bf16[2,512,2048]{2,1,0:T(8,128)(2,1)}, bf16[2,512,2048]{2,1,0:T(8,128)(2,1)S(1)}, u32[]{:S(2)}) copy-start(bf16[2,512,2048]{2,1,0:T(8,128)(2,1)S(1)} %maximum_convert_fusion) | copy-start | bytes 12582916
  101.2 2.0 copy-start.4
  239.0 8.5 %copy-start.5 = (bf16[2,512,2048]{2,1,0:T(8,128)(2,1)S(1)}, bf16[2,512,2048]{2,1,0:T(8,128)(2,1)}, u32[]{:S(2)}) copy-start(bf16[2,512,2048]{2,1,0:T(8,128)(2,1)} %copy-done.4) | copy-start | bytes 12582916
  247.6 8.5 %copy-start.2 = (f32[1,512,2048]{2,1,0:T(8,128)}, f32[1,512,2048]{2,1,0:T(8,128)S(1)}, u32[]{:S(2)}) copy-start(f32[1,512,2048]{2,1,0:T(8,128)S(1)} %convolution_bitcast_fusion) | copy-start | bytes 12582916
  256.1 6.1 copy-start.3
  650.6 18.4 %slice-start = ((s8[16777216]{0:T(1024)(128)(4,1)}), s8[4194304]{0:T(1024)(128)(4,1)S(1)}, s32[]{:S(2)}) async-start(s8[16777216]{0:T(1024)(128)(4,1)} %bitcast.55), calls=%async_computation | async-start | bytes 8388608
  655.4 13.6 %slice-start.1 = ((s8[16777216]{0:T(1024)(128)(4,1)}), s8[4194304]{0:T(1024)(128)(4,1)S(1)}, s32[]{:S(2)}) async-start(s8[16777216]{0:T(1024)(128)(4,1)} %bitcast.55), calls=%async_computation.1 | async-start | bytes 8388608
  655.4 13.6 %slice-start.2 = ((s8[16777216]{0:T(1024)(128)(4,1)}), s8[4194304]{0:T(1024)(128)(4,1)S(1)}, s32[]{:S(2)}) async-start(s8[16777216]{0:T(1024)(128)(4,1)} %bitcast.55), calls=%async_computation.2 | async-start | bytes 8388608
  655.4 15.3 %slice-start.3 = ((s8[16777216]{0:T(1024)(128)(4,1)}), s8[4194304]{0:T(1024)(128)(4,1)S(1)}, s32[]{:S(2)}) async-start(s8[16777216]{0:T(1024)(128)(4,1)} %bitcast.55), calls=%async_computation.3 | async-start | bytes 8388608

commit v3 on v2

--- a/solution.py
+++ b/solution.py
@@ -105,9 +105,12 @@
 
 TAPER = (32, 64, 96)
 RING = 1024
-
-
-def chunk_plan(row_counts, late):
+ORDERS = (('x', 'y', 'z'), ('y', 'x', 'z'), ('x', 'z', 'y'), ('y', 'z', 'x'))
+SHARES = {4: {128: (40, 40, 24, 24)}, 2: {128: (48, 48, 16, 16), 96: (32, 32, 16, 16), 64: (32, 32, 0, 0), 32: (16, 16, 0, 0)}}
+MIXED = (1,)
+
+
+def chunk_plan(row_counts, itemsize):
     plan, base = [], 0
     for a, rows in enumerate(row_counts):
         left = rows // 2
@@ -116,7 +119,9 @@
         left -= sum(head) + sum(tail)
         row = 0
         for size in head + [CHUNK] * (left // CHUNK) + ([left % CHUNK] if left % CHUNK else []) + tail:
-            plan.append((a, row, base % RING, size // 2, 1 if len(plan) % late == late - 1 else 0))
+            two = (size // 2, size // 2, 0, 0)
+            mixed = len(row_counts) == 1 or a in MIXED
+            plan.append((a, row, base % RING, size, SHARES[itemsize].get(size, two) if mixed else two))
             row, base = row + size, base + size
     return plan
 
@@ -149,25 +154,27 @@
     hooks = work(extra + refs[10:]) if work else {}
     chunks = len(plan)
     sends = {}
-    order = lambda kind, j: (('x', 'y', 'z'), ('y', 'x', 'z'))[j] if kind == 0 else (('x', 'z', 'y'), ('y', 'z', 'x'))[j]
+    parts_of = lambda k: [j for j in range(4) if plan[k][4][j]]
+    align = 16 if make_grad else 8
     state = {}
 
     def start(k):
-        a, row, base, size, _ = plan[k]
+        a, row, base, size, shares = plan[k]
         sends[k] = []
         for old in list(sends):
-            if old < k and plan[old][2] < base + 2 * size and base < plan[old][2] + 2 * plan[old][3]:
+            if old < k and plan[old][2] < base + size and base < plan[old][2] + plan[old][3]:
                 finish(old)
         half = row_counts[a] // 2
-        mine = pl.ds(pl.multiple_of(c * half + row, 16), 2 * size)
-        theirs = pl.ds(pl.multiple_of((1 - c) * half + row, 16), 2 * size)
-        load = pltpu.make_async_copy(parts[a].at[mine], own.at[pl.ds(base, 2 * size)], local_sem.at[k, 2])
+        mine = pl.ds(pl.multiple_of(c * half + row, 16), size)
+        theirs = pl.ds(pl.multiple_of((1 - c) * half + row, 16), size)
+        load = pltpu.make_async_copy(parts[a].at[mine], own.at[pl.ds(base, size)], local_sem.at[k, 4])
         load.start()
-        copy = remote(parts[a].at[theirs], from_core.at[pl.ds(base, 2 * size)], core_send.at[k, 0], core_recv.at[k, 0], core_peer)
+        copy = remote(parts[a].at[theirs], from_core.at[pl.ds(base, size)], core_send.at[k, 0], core_recv.at[k, 0], core_peer)
         sends[k].append(copy)
         state[k] = {'load': load, 'core': copy}
-        for j in range(2):
-            state[k, j] = dict(rows=pl.ds(base + j * size, size), out=row + j * size, size=size, col=0, cols=WIDTH)
+        for j in parts_of(k):
+            skip = sum(shares[:j])
+            state[k, j] = dict(rows=pl.ds(base + skip, shares[j]), out=row + skip, size=shares[j], col=0, cols=WIDTH)
 
     def finish(k):
         state[k]['pair'].wait_recv()
@@ -181,7 +188,7 @@
         return s['rows'], columns(s)
 
     def scatter(k, j, step):
-        dims = order(plan[k][4], j)
+        dims = ORDERS[j]
         dim = dims[step]
         s = state[k, j]
         base = 0 if step == 0 else (1 if step == 1 else 2 if dims[1] != 'z' else 4)
@@ -211,23 +218,23 @@
         _, _, base, size, _ = plan[k]
         state[k]['load'].wait()
         state[k]['core'].wait_recv()
-        rows = pl.ds(base, 2 * size)
+        rows = pl.ds(base, size)
         own[rows] = own[rows] + from_core[rows]
-        for j in range(2):
+        for j in parts_of(k):
             scatter(k, j, 0)
 
     def middle(step, k):
-        for j in range(2):
+        for j in parts_of(k):
             own[at(state[k, j])] = absorb(k, j)
             scatter(k, j, step)
 
     def out_at(k, s):
         a = plan[k][0]
         row = c * (row_counts[a] // 2) + s['out']
-        return outs[a].at[pl.ds(pl.multiple_of(row, 16), s['size']), columns(s)]
+        return outs[a].at[pl.ds(pl.multiple_of(row, align), s['size']), columns(s)]
 
     def gather(k, j, step):
-        dims = order(plan[k][4], j)
+        dims = ORDERS[j]
         dim = dims[2 - step]
         s = state[k, j]
         base = 5 + (0 if step == 0 else 4 if step == 2 else (1 if dims[2] != 'z' else 3))
@@ -242,7 +249,7 @@
 
     def turn(k):
         a = plan[k][0]
-        for j in range(2):
+        for j in parts_of(k):
             s = state[k, j]
             total = absorb(k, j)
             if make_grad:
@@ -264,7 +271,7 @@
             gather(k, j, 0)
 
     def spread(step, k):
-        for j in range(2):
+        for j in parts_of(k):
             s = state[k, j]
             for copy in s['copies']:
                 copy.wait_recv()
@@ -274,17 +281,17 @@
 
     def pair(k):
         a, row, _, size, _ = plan[k]
-        for j in range(2):
+        for j in parts_of(k):
             for copy in state[k, j]['copies']:
                 copy.wait_recv()
-        rows = pl.ds(pl.multiple_of(c * (row_counts[a] // 2) + row, 16), 2 * size)
+        rows = pl.ds(pl.multiple_of(c * (row_counts[a] // 2) + row, 16), size)
         copy = remote(outs[a].at[rows], outs[a].at[rows], core_send.at[k, 1], core_recv.at[k, 1], core_peer)
         sends[k].append(copy)
         state[k]['pair'] = copy
 
     stages = [first, functools.partial(middle, 1), functools.partial(middle, 2), turn, functools.partial(spread, 1), functools.partial(spread, 2), pair]
     for t in range(chunks + len(stages) - 1):
-        for task in hooks.get(t, ()):
+        for task in hooks.get(t, ()) if t == 0 else ():
             task()
         for k in range(chunks):
             if t == (max(k - 1, 0) if work and k >= len(TAPER) else 0):
@@ -292,13 +299,16 @@
         for i, stage in enumerate(stages):
             if 0 <= t - i < chunks:
                 stage(t - i)
+            if i == 2 and t:
+                for task in hooks.get(t, ()):
+                    task()
     for k in list(sends):
         finish(k)
 
 
-def reduce_all(parts, collective_id, lam=None, num_rows=None, late=3):
+def reduce_all(parts, collective_id, lam=None, num_rows=None):
     row_counts = [p.shape[0] for p in parts]
-    plan = chunk_plan(row_counts, late)
+    plan = chunk_plan(row_counts, 2 if lam is not None else 4)
     chunks, rows = len(plan), sum(row_counts) // 2
     any_spec = pl.BlockSpec(memory_space=pl.ANY)
     make_grad = lam is not None
@@ -316,8 +326,8 @@
     scratch = [
         pltpu.VMEM((rows, WIDTH), f32), pltpu.VMEM((rows, WIDTH), f32), pltpu.VMEM((rows, WIDTH // 2), f32),
         pltpu.VMEM((rows, 3 * WIDTH // 8), f32), pltpu.VMEM((rows, 3 * WIDTH // 16), f32),
-        pltpu.SemaphoreType.DMA((chunks, 2, 10)), pltpu.SemaphoreType.DMA((chunks, 2, 10)),
-        pltpu.SemaphoreType.DMA((chunks, 2)), pltpu.SemaphoreType.DMA((chunks, 2)), pltpu.SemaphoreType.DMA((chunks, 3)),
+        pltpu.SemaphoreType.DMA((chunks, 4, 10)), pltpu.SemaphoreType.DMA((chunks, 4, 10)),
+        pltpu.SemaphoreType.DMA((chunks, 2)), pltpu.SemaphoreType.DMA((chunks, 2)), pltpu.SemaphoreType.DMA((chunks, 5)),
     ]
     if make_grad:
         scratch.append(pltpu.VMEM((rows, WIDTH // 16), jnp.bfloat16))
@@ -429,16 +439,16 @@
     return {
         0: [grad_load.wait, run(weight_grad, hid_two, part_third, 0, 2)], 1: [run(weight_grad, hid_two, part_third, 2, 4)],
         2: [run(weight_grad, hid_two, part_third, 4, 8)], 3: [run(input_grad, 1, 0, 4)], 4: [run(input_grad, 1, 4, 8), step(0, 0)],
-        5: [step(0, 1)], 6: [step(0, 2)], 7: [step(0, 3)], 8: [step(0, 4), run(norm_grad, 1)],
-        9: [run(weight_grad, hid_one, part_second, 0, 4)], 10: [run(weight_grad, hid_one, part_second, 4, 8)],
-        11: [run(input_grad, 0, 0, 4)], 12: [run(input_grad, 0, 4, 8), step(1, 0)],
-        13: [step(1, 1)], 14: [step(1, 2)], 15: [step(1, 3)], 16: [step(1, 4), run(norm_grad, 0)], 17: [run(weight_grad, feats, part_first, 0, 2)],
+        5: [step(0, 1)], 6: [step(0, 2)], 7: [step(0, 3)], 8: [step(0, 4), run(norm_grad, 1), run(weight_grad, hid_one, part_second, 0, 2)],
+        9: [run(weight_grad, hid_one, part_second, 2, 8)],
+        10: [run(input_grad, 0, 0, 4)], 11: [run(input_grad, 0, 4, 8), step(1, 0)],
+        12: [step(1, 1)], 13: [step(1, 2)], 14: [step(1, 3)], 15: [step(1, 4), run(norm_grad, 0)], 16: [run(weight_grad, feats, part_first, 0, 2)],
     }
 
 
 def reduce_with_backward(work_inputs, collective_id, num_rows):
     row_counts = [WIDTH, WIDTH, WIDTH // 4]
-    plan = chunk_plan(row_counts, 3)
+    plan = chunk_plan(row_counts, 4)
     chunks, rows, views = len(plan), RING, 2 * VIEW_ROWS
     any_spec, vmem_spec = pl.BlockSpec(memory_space=pl.ANY), pl.BlockSpec(memory_space=pltpu.VMEM)
     f32, bf16, dma = jnp.float32, jnp.bfloat16, pltpu.SemaphoreType.DMA
@@ -447,7 +457,7 @@
     scratch = [
         pltpu.VMEM((rows, WIDTH), f32), pltpu.VMEM((rows, WIDTH), f32), pltpu.VMEM((rows, WIDTH // 2), f32),
         pltpu.VMEM((rows, 3 * WIDTH // 8), f32), pltpu.VMEM((rows, 3 * WIDTH // 16), f32),
-        dma((chunks, 2, 10)), dma((chunks, 2, 10)), dma((chunks, 2)), dma((chunks, 2)), dma((chunks, 3)),
+        dma((chunks, 4, 10)), dma((chunks, 4, 10)), dma((chunks, 2)), dma((chunks, 2)), dma((chunks, 5)),
         pltpu.VMEM((views, WIDTH), bf16), pltpu.VMEM((views, WIDTH), f32), pltpu.VMEM((2, TILE, WIDTH), bf16), pltpu.VMEM((2, views, TILE), f32),
         pltpu.VMEM((2, views, TILE), bf16), pltpu.VMEM((2, TILE, WIDTH), f32),
         *stat, *stat, dma, dma((2,)), dma((2,)), dma((2,)), dma((2,)),

time: 682 us -> 649 us (0.952)
  Pallas kernels: 540 us -> 507 us
    pallas_call x1, Pallas kernels: 362 us -> 337 us  [reduce_with_backward(): pl.pallas_call(functools.partial(reduce_kernel, row_counts, plan, None, f...]
    pallas_call x1, Pallas kernels: 126 us -> 118 us  [reduce_all(): pl.pallas_call(functools.partial(reduce_kernel, row_counts, plan, num_row...]
where the time goes in v3:
time: 649 us; the launch traced here: 645 us
  Pallas kernels  507 us (78%)
  matrix products  63.2 us (10%)
  other arithmetic  41 us (6%)
  local copies, waits for them, and re-layouts  30.9 us (5%)
    pallas_call x1, Pallas kernels, reduce_with_backward(): pl.pallas_call(functools.partial(reduce_kernel, row_counts, plan, None, f...  337 us
    pallas_call x1, Pallas kernels, reduce_all(): pl.pallas_call(functools.partial(reduce_kernel, row_counts, plan, num_row...  118 us
    pallas_call x4, Pallas kernels, sum_stats(): pl.pallas_call(functools.partial(stat_kernel, half), out_shape=jax.ShapeD...  52.8 us
    unnamed x31, local copies, waits for them, and re-layouts  28.4 us
    dot_general x2, matrix products, run_layer(): jnp.einsum('vnf,fd->vnd', hidden, weight, preferred_element_type=jnp.floa...  22.6 us
    dot_general x1, matrix products, device_step(): jnp.einsum('vnf,fd->vnd', hid_two, w_third, preferred_element_type=jnp.fl...  14.9 us

profile of v3, /device:TPU:0, one launch (start us, length us, event | category | flops | bytes accessed | tf_op | source)
XLA Modules:
  0.0 644.6 jit_solution(161190669154469180)
XLA Ops:
  1.3 2.4 pad_maximum_fusion
  3.6 7.7 %fusion.17 = (f32[2,2048]{1,0:T(2,128)S(1)}, f32[2,2048]{1,0:T(2,128)S(1)}, f32[2,512,2048]{2,1,0:T(8,128)}) fusion(bf16[512,2048]{1,0:T(8,128)(2,1)} %param.12, bf16[1,512,512]{2,1,0:T(8,128)(2,1)} %bitcast.59, bf16[1,512,512]{2,1,0:T(8,128)(2,1)} %bitcast.61), kind=kOutput, calls=%fused_computation.47 | convolution fusion | flops 2154291200 | bytes 11567104 | tf_op jit(solution)/shard_map/vnf,fd->vnd/dot_general | solution.py:486
  11.4 0.6 pad_maximum_fusion.1.refs_0_
  12.0 14.9 %shard_map.161 = f32[4,2048]{1,0:T(4,128)} custom-call(f32[4,2048]{1,0:T(4,128)} %pad_maximum_fusion.1.refs_0_), custom_call_target="tpu_custom_call" | custom-call | tf_op jit(solution)/shard_map/pallas_call | solution.py:95
  26.9 0.8 broadcast_multiply_fusion.2
  27.7 0.0 copy-done.6
  27.7 0.0 copy-done.7
  27.7 4.9 maximum_convert_fusion.1
  32.6 0.0 copy-start
  32.6 0.0 copy-start.8
  32.7 0.0 copy-start.9
  32.7 14.8 %fusion.16 = (f32[2,2048]{1,0:T(2,128)S(1)}, f32[2,2048]{1,0:T(2,128)S(1)}, f32[2,512,2048]{2,1,0:T(8,128)}) fusion(bf16[2,512,2048]{2,1,0:T(8,128)(2,1)S(1)} %maximum_convert_fusion.1, bf16[2048,2048]{1,0:T(8,128)(2,1)} %refs_3_.1), kind=kOutput, calls=%fused_computation.46 | convolution fusion | flops 8596217856 | bytes 21004288 | tf_op jit(solution)/shard_map/vnf,fd->vnd/dot_general | solution.py:486
  47.5 0.0 copy-done
  47.5 0.6 pad_maximum_fusion.2.refs_0_
  48.2 12.9 %shard_map.162 = f32[4,2048]{1,0:T(4,128)} custom-call(f32[4,2048]{1,0:T(4,128)} %pad_maximum_fusion.2.refs_0_), custom_call_target="tpu_custom_call" | custom-call | tf_op jit(solution)/shard_map/pallas_call | solution.py:95
  61.0 0.8 broadcast_multiply_fusion.1
  61.8 0.0 copy-done.8
  61.8 0.0 copy-done.9
  61.8 1.4 concatenate.23.refs_8_
  63.2 4.9 maximum_convert_fusion
  68.1 0.0 copy-start.1
  68.1 14.9 %fusion.15 = (f32[2,2048]{1,0:T(2,128)S(1)}, f32[2,2048]{1,0:T(2,128)S(1)}, f32[2,512,2048]{2,1,0:T(8,128)}) fusion(bf16[2,512,2048]{2,1,0:T(8,128)(2,1)S(1)} %maximum_convert_fusion, bf16[2048,2048]{1,0:T(8,128)(2,1)} %refs_2_.1), kind=kOutput, calls=%fused_computation.45 | convolution fusion | flops 8596217856 | bytes 21004288 | tf_op jit(solution)/shard_map/vnf,fd->vnd/dot_general | solution.py:497
  83.1 0.6 pad_maximum_fusion.3.refs_0_
  83.7 12.1 %shard_map.163 = f32[4,2048]{1,0:T(4,128)} custom-call(f32[4,2048]{1,0:T(4,128)} %pad_maximum_fusion.3.refs_0_), custom_call_target="tpu_custom_call" | custom-call | tf_op jit(solution)/shard_map/pallas_call | solution.py:95
  95.8 0.8 broadcast_multiply_fusion
  96.6 4.6 fusion.4
  101.2 0.0 copy-start.4
  101.2 2.0 copy-done.4
  103.2 8.7 %fusion.8.refs_0_ = f32[2048,2048]{1,0:T(8,128)} fusion(bf16[2,512,2048]{2,1,0:T(8,128)(2,1)S(1)} %fusion.4), kind=kOutput, calls=%fused_computation.21 | convolution fusion | flops 4294967296 | bytes 20971520 | tf_op jit(solution)/shard_map/dot_general | solution.py:501
  111.9 117.6 %shard_map.164 = (bf16[2048,2048]{1,0:T(8,128)(2,1)}, f32[8,128]{1,0:T(8,128)}) custom-call(f32[2048,2048]{1,0:T(8,128)} %fusion.8.refs_0_, f32[1,1]{1,0:T(1,128)} %bitcast.49.refs_1_), custom_call_target="tpu_custom_call" | custom-call | tf_op jit(solution)/shard_map/pallas_call | solution.py:334
  229.5 1.3 reduce_sum.89
  230.8 8.5 %convolution_bitcast_fusion = f32[1,512,2048]{2,1,0:T(8,128)S(1)} fusion(bf16[2048,2048]{1,0:T(8,128)(2,1)} %get-tuple-element.15, bf16[2,512,2048]{2,1,0:T(8,128)(2,1)} %copy-done.4), kind=kOutput, calls=%fused_computation.15 | convolution fusion | flops 4294967296 | bytes 14680064 | tf_op jit(solution)/shard_map/dot_general | solution.py:504
  239.4 0.0 copy-start.2
  239.4 8.5 %convolution_bitcast_fusion.1 = f32[1,512,2048]{2,1,0:T(8,128)S(1)} fusion(bf16[2048,2048]{1,0:T(8,128)(2,1)} %get-tuple-element.15, bf16[2,512,2048]{2,1,0:T(8,128)(2,1)S(1)} %copy-done.5), kind=kOutput, calls=%fused_computation.16 | convolution fusion | flops 4294967296 | bytes 14680064 | tf_op jit(solution)/shard_map/dot_general | solution.py:503
  247.9 0.0 copy-start.3
  247.9 6.1 fusion.5
  254.0 1.3 select_maximum_fusion.refs_0_
  255.2 13.0 %shard_map.165 = f32[4,2304]{1,0:T(4,128)} custom-call(f32[4,2304]{1,0:T(4,128)} %select_maximum_fusion.refs_0_), custom_call_target="tpu_custom_call" | custom-call | tf_op jit(solution)/shard_map/pallas_call | solution.py:95
  268.2 1.2 slice.86
  269.4 0.8 slice_multiply_fusion
  270.2 9.0 %multiply_convert_fusion = bf16[2,512,2048]{2,1,0:T(8,128)(2,1)} fusion(f32[2,512,2048]{2,1,0:T(8,128)} %get-tuple-element.44, f32[1,512,2048]{2,1,0:T(8,128)} %copy-done.2, f32[1,512,2048]{2,1,0:T(8,128)} %copy-done.3, f32[2,2048]{1,0:T(2,128)S(1)} %get-tuple-element.35, f32[2,2048]{1,0:T(2,128)S(1)} %get-tuple-element.34, ...), kind=kLoop, calls=%fused_computation.5 | loop fusion | flops 18874368 | bytes 21037056 | tf_op jit(solution)/shard_map/convert_element_type | solution.py:511
  279.2 337.0 %shard_map.166 = (f32[2048,2048]{1,0:T(8,128)}, f32[2048,2048]{1,0:T(8,128)}, f32[512,2048]{1,0:T(8,128)}, f32[2048,2048]{1,0:T(8,128)}, f32[2048,2048]{1,0:T(8,...) custom-call(bf16[1024,2048]{1,0:T(8,128)(2,1)} %bitcast.52, bf16[1024,2048]{1,0:T(8,128)(2,1)} %bitcast.54, ...), custom_call_target="tpu_custom_call" | custom-call | tf_op jit(solution)/shard_map/pallas_call | solution.py:466
  616.1 1.6 slice_add_fusion
  617.8 4.8 copy.22
  622.6 13.6 %copy.23 = f32[2048,2048]{1,0:T(8,128)} copy(f32[2048,2048]{1,0:T(8,128)} %get-tuple-element.57) | data formatting | bytes 33554432
  636.2 0.0 slice-done.1
  636.2 1.7 slice-done.3
  638.0 6.2 copy.24
  (18 shorter events, 0.1 us)
Async XLA Ops:
  3.6 24.1 %copy-start.6 = (f32[2048]{0:T(1024)S(1)}, f32[2048]{0:T(1024)}, u32[]{:S(2)}) copy-start(f32[2048]{0:T(1024)} %param.16) | copy-start | bytes 24580
  3.6 24.1 %copy-start.7 = (f32[2048]{0:T(1024)S(1)}, f32[2048]{0:T(1024)}, u32[]{:S(2)}) copy-start(f32[2048]{0:T(1024)} %param.15) | copy-start | bytes 24580
  32.6 14.9 %copy-start = (bf16[2,512,2048]{2,1,0:T(8,128)(2,1)}, bf16[2,512,2048]{2,1,0:T(8,128)(2,1)S(1)}, u32[]{:S(2)}) copy-start(bf16[2,512,2048]{2,1,0:T(8,128)(2,1)S(1)} %maximum_convert_fusion.1) | copy-start | bytes 12582916
  32.6 29.2 %copy-start.8 = (f32[2048]{0:T(1024)S(1)}, f32[2048]{0:T(1024)}, u32[]{:S(2)}) copy-start(f32[2048]{0:T(1024)} %param.18) | copy-start | bytes 24580
  32.7 29.2 %copy-start.9 = (f32[2048]{0:T(1024)S(1)}, f32[2048]{0:T(1024)}, u32[]{:S(2)}) copy-start(f32[2048]{0:T(1024)} %param.17) | copy-start | bytes 24580
  68.1 14.9 %copy-start.1 = (bf16[2,512,2048]{2,1,0:T(8,128)(2,1)}, bf16[2,512,2048]{2,1,0:T(8,128)(2,1)S(1)}, u32[]{:S(2)}) copy-start(bf16[2,512,2048]{2,1,0:T(8,128)(2,1)S(1)} %maximum_convert_fusion) | copy-start | bytes 12582916
  101.2 2.0 copy-start.4
  230.8 8.5 %copy-start.5 = (bf16[2,512,2048]{2,1,0:T(8,128)(2,1)S(1)}, bf16[2,512,2048]{2,1,0:T(8,128)(2,1)}, u32[]{:S(2)}) copy-start(bf16[2,512,2048]{2,1,0:T(8,128)(2,1)} %copy-done.4) | copy-start | bytes 12582916
  239.4 8.5 %copy-start.2 = (f32[1,512,2048]{2,1,0:T(8,128)}, f32[1,512,2048]{2,1,0:T(8,128)S(1)}, u32[]{:S(2)}) copy-start(f32[1,512,2048]{2,1,0:T(8,128)S(1)} %convolution_bitcast_fusion) | copy-start | bytes 12582916
  247.9 6.1 copy-start.3
  617.8 18.4 %slice-start = ((s8[16777216]{0:T(1024)(128)(4,1)}), s8[4194304]{0:T(1024)(128)(4,1)S(1)}, s32[]{:S(2)}) async-start(s8[16777216]{0:T(1024)(128)(4,1)} %bitcast.55), calls=%async_computation | async-start | bytes 8388608
  622.6 13.6 %slice-start.1 = ((s8[16777216]{0:T(1024)(128)(4,1)}), s8[4194304]{0:T(1024)(128)(4,1)S(1)}, s32[]{:S(2)}) async-start(s8[16777216]{0:T(1024)(128)(4,1)} %bitcast.55), calls=%async_computation.1 | async-start | bytes 8388608
  622.6 13.6 %slice-start.2 = ((s8[16777216]{0:T(1024)(128)(4,1)}), s8[4194304]{0:T(1024)(128)(4,1)S(1)}, s32[]{:S(2)}) async-start(s8[16777216]{0:T(1024)(128)(4,1)} %bitcast.55), calls=%async_computation.2 | async-start | bytes 8388608
  622.6 15.3 %slice-start.3 = ((s8[16777216]{0:T(1024)(128)(4,1)}), s8[4194304]{0:T(1024)(128)(4,1)S(1)}, s32[]{:S(2)}) async-start(s8[16777216]{0:T(1024)(128)(4,1)} %bitcast.55), calls=%async_computation.3 | async-start | bytes 8388608

commit v4 on v3

--- a/solution.py
+++ b/solution.py
@@ -114,7 +114,7 @@
     plan, base = [], 0
     for a, rows in enumerate(row_counts):
         left = rows // 2
-        head = list(TAPER) if a == 0 else []
+        head = [] if a else list(TAPER) if len(row_counts) == 1 else [64]
         tail = list(TAPER[::-1]) if a == len(row_counts) - 1 else []
         left -= sum(head) + sum(tail)
         row = 0
@@ -291,15 +291,15 @@
 
     stages = [first, functools.partial(middle, 1), functools.partial(middle, 2), turn, functools.partial(spread, 1), functools.partial(spread, 2), pair]
     for t in range(chunks + len(stages) - 1):
-        for task in hooks.get(t, ()) if t == 0 else ():
+        for task in hooks.get(-1, ()) if t == 0 else ():
             task()
         for k in range(chunks):
-            if t == (max(k - 1, 0) if work and k >= len(TAPER) else 0):
+            if t == (k - 1 if work and k else 0):
                 start(k)
         for i, stage in enumerate(stages):
             if 0 <= t - i < chunks:
                 stage(t - i)
-            if i == 2 and t:
+            if i == 2:
                 for task in hooks.get(t, ()):
                     task()
     for k in list(sends):
@@ -437,12 +437,12 @@
     step = lambda which, i: functools.partial(sums[which].step, i)
     run = functools.partial
     return {
-        0: [grad_load.wait, run(weight_grad, hid_two, part_third, 0, 2)], 1: [run(weight_grad, hid_two, part_third, 2, 4)],
-        2: [run(weight_grad, hid_two, part_third, 4, 8)], 3: [run(input_grad, 1, 0, 4)], 4: [run(input_grad, 1, 4, 8), step(0, 0)],
-        5: [step(0, 1)], 6: [step(0, 2)], 7: [step(0, 3)], 8: [step(0, 4), run(norm_grad, 1), run(weight_grad, hid_one, part_second, 0, 2)],
-        9: [run(weight_grad, hid_one, part_second, 2, 8)],
-        10: [run(input_grad, 0, 0, 4)], 11: [run(input_grad, 0, 4, 8), step(1, 0)],
-        12: [step(1, 1)], 13: [step(1, 2)], 14: [step(1, 3)], 15: [step(1, 4), run(norm_grad, 0)], 16: [run(weight_grad, feats, part_first, 0, 2)],
+        -1: [grad_load.wait, run(weight_grad, hid_two, part_third, 0, 2)], 0: [run(weight_grad, hid_two, part_third, 2, 4)],
+        1: [run(weight_grad, hid_two, part_third, 4, 8)], 2: [run(input_grad, 1, 0, 4)], 3: [run(input_grad, 1, 4, 8), step(0, 0)],
+        4: [step(0, 1)], 5: [step(0, 2)], 6: [step(0, 3)], 7: [step(0, 4), run(norm_grad, 1), run(weight_grad, hid_one, part_second, 0, 2)],
+        8: [run(weight_grad, hid_one, part_second, 2, 8)],
+        9: [run(input_grad, 0, 0, 4)], 10: [run(input_grad, 0, 4, 8), step(1, 0)],
+        11: [step(1, 1)], 12: [step(1, 2)], 13: [step(1, 3)], 14: [step(1, 4), run(norm_grad, 0)], 15: [run(weight_grad, feats, part_first, 0, 2)],
     }
 
 

time: 649 us -> 648 us (level)
  no operation moved by 1% of the time
where the time goes in v4:
time: 648 us; the launch traced here: 640 us
  Pallas kernels  503 us (78%)
  matrix products  63.2 us (10%)
  other arithmetic  41 us (6%)
  local copies, waits for them, and re-layouts  30.9 us (5%)
    pallas_call x1, Pallas kernels, reduce_with_backward(): pl.pallas_call(functools.partial(reduce_kernel, row_counts, plan, None, f...  332 us
    pallas_call x1, Pallas kernels, reduce_all(): pl.pallas_call(functools.partial(reduce_kernel, row_counts, plan, num_row...  118 us
    pallas_call x4, Pallas kernels, sum_stats(): pl.pallas_call(functools.partial(stat_kernel, half), out_shape=jax.ShapeD...  52.8 us
    unnamed x31, local copies, waits for them, and re-layouts  28.4 us
    dot_general x2, matrix products, run_layer(): jnp.einsum('vnf,fd->vnd', hidden, weight, preferred_element_type=jnp.floa...  22.6 us
    dot_general x1, matrix products, device_step(): jnp.einsum('vnf,fd->vnd', hid_two, w_third, preferred_element_type=jnp.fl...  14.9 us

profile of v4, /device:TPU:0, one launch (start us, length us, event | category | flops | bytes accessed | tf_op | source)
XLA Modules:
  0.0 639.8 jit_solution(14078776355988006599)
XLA Ops:
  1.3 2.4 pad_maximum_fusion
  3.6 7.7 %fusion.17 = (f32[2,2048]{1,0:T(2,128)S(1)}, f32[2,2048]{1,0:T(2,128)S(1)}, f32[2,512,2048]{2,1,0:T(8,128)}) fusion(bf16[512,2048]{1,0:T(8,128)(2,1)} %param.12, bf16[1,512,512]{2,1,0:T(8,128)(2,1)} %bitcast.59, bf16[1,512,512]{2,1,0:T(8,128)(2,1)} %bitcast.61), kind=kOutput, calls=%fused_computation.47 | convolution fusion | flops 2154291200 | bytes 11567104 | tf_op jit(solution)/shard_map/vnf,fd->vnd/dot_general | solution.py:486
  11.4 0.6 pad_maximum_fusion.1.refs_0_
  12.0 14.9 %shard_map.161 = f32[4,2048]{1,0:T(4,128)} custom-call(f32[4,2048]{1,0:T(4,128)} %pad_maximum_fusion.1.refs_0_), custom_call_target="tpu_custom_call" | custom-call | tf_op jit(solution)/shard_map/pallas_call | solution.py:95
  26.9 0.8 broadcast_multiply_fusion.2
  27.7 0.0 copy-done.6
  27.7 0.0 copy-done.7
  27.7 4.9 maximum_convert_fusion.1
  32.6 0.0 copy-start
  32.6 0.0 copy-start.8
  32.7 0.0 copy-start.9
  32.7 14.8 %fusion.16 = (f32[2,2048]{1,0:T(2,128)S(1)}, f32[2,2048]{1,0:T(2,128)S(1)}, f32[2,512,2048]{2,1,0:T(8,128)}) fusion(bf16[2,512,2048]{2,1,0:T(8,128)(2,1)S(1)} %maximum_convert_fusion.1, bf16[2048,2048]{1,0:T(8,128)(2,1)} %refs_3_.1), kind=kOutput, calls=%fused_computation.46 | convolution fusion | flops 8596217856 | bytes 21004288 | tf_op jit(solution)/shard_map/vnf,fd->vnd/dot_general | solution.py:486
  47.5 0.0 copy-done
  47.5 0.6 pad_maximum_fusion.2.refs_0_
  48.2 12.9 %shard_map.162 = f32[4,2048]{1,0:T(4,128)} custom-call(f32[4,2048]{1,0:T(4,128)} %pad_maximum_fusion.2.refs_0_), custom_call_target="tpu_custom_call" | custom-call | tf_op jit(solution)/shard_map/pallas_call | solution.py:95
  61.0 0.8 broadcast_multiply_fusion.1
  61.8 0.0 copy-done.8
  61.8 0.0 copy-done.9
  61.8 1.4 concatenate.23.refs_8_
  63.2 4.9 maximum_convert_fusion
  68.1 14.9 %fusion.15 = (f32[2,2048]{1,0:T(2,128)S(1)}, f32[2,2048]{1,0:T(2,128)S(1)}, f32[2,512,2048]{2,1,0:T(8,128)}) fusion(bf16[2,512,2048]{2,1,0:T(8,128)(2,1)S(1)} %maximum_convert_fusion, bf16[2048,2048]{1,0:T(8,128)(2,1)} %refs_2_.1), kind=kOutput, calls=%fused_computation.45 | convolution fusion | flops 8596217856 | bytes 21004288 | tf_op jit(solution)/shard_map/vnf,fd->vnd/dot_general | solution.py:497
  83.1 0.6 pad_maximum_fusion.3.refs_0_
  83.7 12.1 %shard_map.163 = f32[4,2048]{1,0:T(4,128)} custom-call(f32[4,2048]{1,0:T(4,128)} %pad_maximum_fusion.3.refs_0_), custom_call_target="tpu_custom_call" | custom-call | tf_op jit(solution)/shard_map/pallas_call | solution.py:95
  95.8 0.8 broadcast_multiply_fusion
  96.6 4.6 fusion.4
  101.2 0.0 copy-start.4
  101.2 2.0 copy-done.4
  103.2 8.7 %fusion.8.refs_0_ = f32[2048,2048]{1,0:T(8,128)} fusion(bf16[2,512,2048]{2,1,0:T(8,128)(2,1)S(1)} %fusion.4), kind=kOutput, calls=%fused_computation.21 | convolution fusion | flops 4294967296 | bytes 20971520 | tf_op jit(solution)/shard_map/dot_general | solution.py:501
  111.9 117.6 %shard_map.164 = (bf16[2048,2048]{1,0:T(8,128)(2,1)}, f32[8,128]{1,0:T(8,128)}) custom-call(f32[2048,2048]{1,0:T(8,128)} %fusion.8.refs_0_, f32[1,1]{1,0:T(1,128)} %bitcast.49.refs_1_), custom_call_target="tpu_custom_call" | custom-call | tf_op jit(solution)/shard_map/pallas_call | solution.py:334
  229.5 1.3 reduce_sum.89
  230.8 8.5 %convolution_bitcast_fusion = f32[1,512,2048]{2,1,0:T(8,128)S(1)} fusion(bf16[2048,2048]{1,0:T(8,128)(2,1)} %get-tuple-element.15, bf16[2,512,2048]{2,1,0:T(8,128)(2,1)} %copy-done.4), kind=kOutput, calls=%fused_computation.15 | convolution fusion | flops 4294967296 | bytes 14680064 | tf_op jit(solution)/shard_map/dot_general | solution.py:504
  239.3 0.0 copy-done.5
  239.4 0.0 copy-start.2
  239.4 8.5 %convolution_bitcast_fusion.1 = f32[1,512,2048]{2,1,0:T(8,128)S(1)} fusion(bf16[2048,2048]{1,0:T(8,128)(2,1)} %get-tuple-element.15, bf16[2,512,2048]{2,1,0:T(8,128)(2,1)S(1)} %copy-done.5), kind=kOutput, calls=%fused_computation.16 | convolution fusion | flops 4294967296 | bytes 14680064 | tf_op jit(solution)/shard_map/dot_general | solution.py:503
  247.9 0.0 copy-start.3
  247.9 6.1 fusion.5
  254.0 1.3 select_maximum_fusion.refs_0_
  255.2 13.0 %shard_map.165 = f32[4,2304]{1,0:T(4,128)} custom-call(f32[4,2304]{1,0:T(4,128)} %select_maximum_fusion.refs_0_), custom_call_target="tpu_custom_call" | custom-call | tf_op jit(solution)/shard_map/pallas_call | solution.py:95
  268.2 1.2 slice.86
  269.4 0.8 slice_multiply_fusion
  270.2 9.0 %multiply_convert_fusion = bf16[2,512,2048]{2,1,0:T(8,128)(2,1)} fusion(f32[2,512,2048]{2,1,0:T(8,128)} %get-tuple-element.44, f32[1,512,2048]{2,1,0:T(8,128)} %copy-done.2, f32[1,512,2048]{2,1,0:T(8,128)} %copy-done.3, f32[2,2048]{1,0:T(2,128)S(1)} %get-tuple-element.35, f32[2,2048]{1,0:T(2,128)S(1)} %get-tuple-element.34, ...), kind=kLoop, calls=%fused_computation.5 | loop fusion | flops 18874368 | bytes 21037056 | tf_op jit(solution)/shard_map/convert_element_type | solution.py:511
  279.2 332.2 %shard_map.166 = (f32[2048,2048]{1,0:T(8,128)}, f32[2048,2048]{1,0:T(8,128)}, f32[512,2048]{1,0:T(8,128)}, f32[2048,2048]{1,0:T(8,128)}, f32[2048,2048]{1,0:T(8,...) custom-call(bf16[1024,2048]{1,0:T(8,128)(2,1)} %bitcast.52, bf16[1024,2048]{1,0:T(8,128)(2,1)} %bitcast.54, ...), custom_call_target="tpu_custom_call" | custom-call | tf_op jit(solution)/shard_map/pallas_call | solution.py:466
  611.4 1.6 slice_add_fusion
  613.0 4.8 copy.22
  617.9 13.6 %copy.23 = f32[2048,2048]{1,0:T(8,128)} copy(f32[2048,2048]{1,0:T(8,128)} %get-tuple-element.57) | data formatting | bytes 33554432
  631.5 0.0 slice-done
  631.5 1.7 slice-done.3
  633.2 6.2 copy.24
  (18 shorter events, 0.1 us)
Async XLA Ops:
  3.6 24.1 %copy-start.6 = (f32[2048]{0:T(1024)S(1)}, f32[2048]{0:T(1024)}, u32[]{:S(2)}) copy-start(f32[2048]{0:T(1024)} %param.16) | copy-start | bytes 24580
  3.6 24.1 %copy-start.7 = (f32[2048]{0:T(1024)S(1)}, f32[2048]{0:T(1024)}, u32[]{:S(2)}) copy-start(f32[2048]{0:T(1024)} %param.15) | copy-start | bytes 24580
  32.6 14.9 %copy-start = (bf16[2,512,2048]{2,1,0:T(8,128)(2,1)}, bf16[2,512,2048]{2,1,0:T(8,128)(2,1)S(1)}, u32[]{:S(2)}) copy-start(bf16[2,512,2048]{2,1,0:T(8,128)(2,1)S(1)} %maximum_convert_fusion.1) | copy-start | bytes 12582916
  32.6 29.2 %copy-start.8 = (f32[2048]{0:T(1024)S(1)}, f32[2048]{0:T(1024)}, u32[]{:S(2)}) copy-start(f32[2048]{0:T(1024)} %param.18) | copy-start | bytes 24580
  32.7 29.2 %copy-start.9 = (f32[2048]{0:T(1024)S(1)}, f32[2048]{0:T(1024)}, u32[]{:S(2)}) copy-start(f32[2048]{0:T(1024)} %param.17) | copy-start | bytes 24580
  68.1 14.9 %copy-start.1 = (bf16[2,512,2048]{2,1,0:T(8,128)(2,1)}, bf16[2,512,2048]{2,1,0:T(8,128)(2,1)S(1)}, u32[]{:S(2)}) copy-start(bf16[2,512,2048]{2,1,0:T(8,128)(2,1)S(1)} %maximum_convert_fusion) | copy-start | bytes 12582916
  101.2 2.0 copy-start.4
  230.8 8.5 %copy-start.5 = (bf16[2,512,2048]{2,1,0:T(8,128)(2,1)S(1)}, bf16[2,512,2048]{2,1,0:T(8,128)(2,1)}, u32[]{:S(2)}) copy-start(bf16[2,512,2048]{2,1,0:T(8,128)(2,1)} %copy-done.4) | copy-start | bytes 12582916
  239.4 8.5 %copy-start.2 = (f32[1,512,2048]{2,1,0:T(8,128)}, f32[1,512,2048]{2,1,0:T(8,128)S(1)}, u32[]{:S(2)}) copy-start(f32[1,512,2048]{2,1,0:T(8,128)S(1)} %convolution_bitcast_fusion) | copy-start | bytes 12582916
  247.9 6.1 copy-start.3
  613.0 18.4 %slice-start = ((s8[16777216]{0:T(1024)(128)(4,1)}), s8[4194304]{0:T(1024)(128)(4,1)S(1)}, s32[]{:S(2)}) async-start(s8[16777216]{0:T(1024)(128)(4,1)} %bitcast.55), calls=%async_computation | async-start | bytes 8388608
  617.9 13.6 %slice-start.1 = ((s8[16777216]{0:T(1024)(128)(4,1)}), s8[4194304]{0:T(1024)(128)(4,1)S(1)}, s32[]{:S(2)}) async-start(s8[16777216]{0:T(1024)(128)(4,1)} %bitcast.55), calls=%async_computation.1 | async-start | bytes 8388608
  617.9 13.6 %slice-start.2 = ((s8[16777216]{0:T(1024)(128)(4,1)}), s8[4194304]{0:T(1024)(128)(4,1)S(1)}, s32[]{:S(2)}) async-start(s8[16777216]{0:T(1024)(128)(4,1)} %bitcast.55), calls=%async_computation.2 | async-start | bytes 8388608
  617.9 15.3 %slice-start.3 = ((s8[16777216]{0:T(1024)(128)(4,1)}), s8[4194304]{0:T(1024)(128)(4,1)S(1)}, s32[]{:S(2)}) async-start(s8[16777216]{0:T(1024)(128)(4,1)} %bitcast.55), calls=%async_computation.3 | async-start | bytes 8388608
